TPU v7x, 32 devices: a whole 2x2x4 slice. The times are simulated.
32 devices in a mesh: lat: 8 (over y, x, core), lon: 4 (over z).
Axes of the slice: x: 2, y: 2, z: 4, core: 2. Of those that a mesh axis runs over, the one named last changes fastest.
Arguments:
- coeffs_old: float32 [640, 2, 3, 50, 640], P(('lat', 'lon')), may hold values from -0.16 to 0.16
- noise: bfloat16 [640, 2, 3, 50, 640], P(('lat', 'lon')), may hold values from -6 to 6
- legendre: float32 [640, 640, 640], P(('lat', 'lon')), may hold values from -0.25 to 0.25
- decay: float32 [3], replicated, may hold values from 0.3 to 0.97
- amplitude: float32 [3, 640], replicated, may hold values from 0.005 to 0.05
- wavenumber_of_slot: int32 [640], replicated, may hold values from 0 to 639, as said below
- lat_order: int32 [640], replicated, may hold values from 0 to 639, each once
Outputs:
- coeffs_new: float32 [640, 2, 3, 50, 640], P(('lat', 'lon'))
- pattern: float32 [640, 50, 1280], P(('lat', 'lon'))
Inputs may be any that keep to these rules, and one draw needn't show every extreme that they name: `wavenumber_of_slot`: every wavenumber fills exactly one slot; the sums of the wavenumbers of one device's 20 slots differ between devices by less than 32. `lat_order`: every latitude stands in exactly one row.
All inputs are finite; a program needn't handle non-finite values.
Results may differ from a plain program's by a relative error of at most 0.0003.
Values sent between devices are 32-bit elements; how exact they have to be, the bound alone decides.
A program may use at most 192 MiB of HBM per device.

v0:
```python
import functools

import jax
import jax.numpy as jnp
from jax import lax
from jax.experimental import pallas as pl
from jax.experimental.pallas import tpu as pltpu
from jax.sharding import PartitionSpec as P

TWO_PI = 6.283185307179586
LANES = 128


def group_size(slots):
    return 4 if slots % 4 == 0 else slots


def split(x):
    high = x.astype(jnp.bfloat16)
    return high, (x - high.astype(jnp.float32)).astype(jnp.bfloat16)


def transform_kernel(order_ref, waves_ref, decay_ref, old_ref, noise_ref, basis_ref, spread_ref, new_ref, send_ref, weights, field):
    group, step = pl.num_programs(1), pl.program_id(1)
    scales, members = old_ref.shape[2], old_ref.shape[3]
    devices, rows, wide = send_ref.shape[1:]
    lat_dev = order_ref.shape[0] // devices

    @pl.when((pl.program_id(0) == 0) & (step == 0))
    def _():
        weights[...] = jnp.zeros_like(weights)

    width = basis_ref.shape[2]
    wave = waves_ref[pl.program_id(0) * group + step]
    live = lax.broadcasted_iota(jnp.int32, (8, width), 1) + wave < width
    shifted = jnp.where(live, pltpu.roll(spread_ref[...], width - wave, axis=1), 0.0)
    for part in range(2):
        total = None
        for scale in range(scales):
            keep = jnp.where(live[:1], decay_ref[scale], 0.0)
            fresh = shifted[scale : scale + 1, :]
            value = keep * old_ref[0, part, scale] + fresh * noise_ref[0, part, scale].astype(jnp.float32)
            new_ref[0, part, scale] = value
            total = value if total is None else total + value
        weights[part * 64 : part * 64 + members, :] = total
    high, low = split(weights[...])
    both = jnp.concatenate([high, low], axis=0)
    basis_high, basis_low = split(basis_ref[0])
    contract = (((1,), (1,)), ((), ()))
    first = lax.dot_general(basis_high, both, contract, preferred_element_type=jnp.float32)
    second = lax.dot_general(basis_low, high, contract, preferred_element_type=jnp.float32)
    product = first[:, :LANES] + first[:, LANES:] + second
    other = pltpu.roll(product, 64, axis=1)
    for index in range(rows // 2):

        @pl.when(step == index)
        def _(index=index):
            field[:, 2 * index, :] = product
            field[:, 2 * index + 1, :] = other

    @pl.when(step == group - 1)
    def _():
        lane = lax.broadcasted_iota(jnp.int32, (rows, LANES), 1)

        def pack(device, carry):
            tiles = [jnp.zeros((rows, LANES), jnp.float32) for _ in range(wide // LANES)]
            for q in range(lat_dev):
                piece = field[order_ref[device * lat_dev + q]]
                start = members * q
                offset = start % LANES
                if offset:
                    piece = pltpu.roll(piece, offset, axis=1)
                tile = start // LANES
                tiles[tile] = jnp.where((lane >= offset) & (lane < offset + members), piece, tiles[tile])
                if offset + members > LANES:
                    tiles[tile + 1] = jnp.where(lane < offset + members - LANES, piece, tiles[tile + 1])
            for index, tile in enumerate(tiles):
                send_ref[0, device, :, index * LANES : (index + 1) * LANES] = tile
            return carry

        lax.fori_loop(0, devices, pack, 0)


def transform(coeffs_old, noise, legendre, spread, decay, waves, lat_order, devices):
    slots, parts, scales, members, width = coeffs_old.shape
    lats = legendre.shape[1]
    group = group_size(slots)
    rows = group * parts
    wide = -(-(lats // devices * members) // LANES) * LANES

    def slot5(g, i, *_):
        return (g * group + i, 0, 0, 0, 0)

    def slot3(g, i, *_):
        return (g * group + i, 0, 0)

    spec = pltpu.PrefetchScalarGridSpec(
        num_scalar_prefetch=3,
        grid=(slots // group, group),
        in_specs=[
            pl.BlockSpec((1, parts, scales, members, width), slot5),
            pl.BlockSpec((1, parts, scales, members, width), slot5),
            pl.BlockSpec((1, lats, width), slot3),
            pl.BlockSpec((8, width), lambda g, i, *_: (0, 0)),
        ],
        out_specs=[
            pl.BlockSpec((1, parts, scales, members, width), slot5),
            pl.BlockSpec((1, devices, rows, wide), lambda g, i, *_: (g, 0, 0, 0)),
        ],
        scratch_shapes=[
            pltpu.VMEM((LANES, width), jnp.float32),
            pltpu.VMEM((lats, rows, LANES), jnp.float32),
        ],
    )
    return pl.pallas_call(
        transform_kernel,
        grid_spec=spec,
        out_shape=[
            jax.ShapeDtypeStruct(coeffs_old.shape, jnp.float32),
            jax.ShapeDtypeStruct((slots // group, devices, rows, wide), jnp.float32),
        ],
        compiler_params=pltpu.CompilerParams(dimension_semantics=("arbitrary", "arbitrary")),
    )(lat_order, waves, decay, coeffs_old, noise, legendre, spread)


def synthesis_table(waves, length):
    column = lax.broadcasted_iota(jnp.int32, (waves.shape[0], length), 1)
    phase = waves[:, None] * column % length
    angle = phase.astype(jnp.float32) * (TWO_PI / length)
    weight = jnp.where(waves == 0, 1.0, 2.0).astype(jnp.float32)[:, None]
    return jnp.stack([weight * jnp.cos(angle), -weight * jnp.sin(angle)], axis=1).reshape(-1, length)


def local(coeffs_old, noise, legendre, decay, amplitude, wavenumber_of_slot, lat_order):
    devices = lax.axis_size("lat") * lax.axis_size("lon")
    me = lax.axis_index("lat") * lax.axis_size("lon") + lax.axis_index("lon")
    slots, parts, scales, members, width = coeffs_old.shape
    lats = legendre.shape[1]
    lons = 2 * lats
    lat_dev = lats // devices
    group = group_size(slots)
    mine = lax.dynamic_slice_in_dim(wavenumber_of_slot, me * slots, slots)
    spread = jnp.pad(amplitude * jnp.sqrt(1.0 - decay * decay)[:, None], ((0, 8 - scales), (0, 0)))
    coeffs_new, send = transform(coeffs_old, noise, legendre, spread, decay, mine, lat_order, devices)
    got = lax.all_to_all(send, ("lat", "lon"), split_axis=1, concat_axis=1, tiled=True)
    ordered = wavenumber_of_slot.reshape(devices, slots // group, group).transpose(1, 0, 2).reshape(-1)
    table = synthesis_table(ordered, lons)
    values = got.reshape(-1, got.shape[-1])
    out = lax.dot_general(values, table, (((0,), (0,)), ((), ())), precision=lax.Precision.HIGH)
    pattern = out[: lat_dev * members].reshape(lat_dev, members, lons)
    return (coeffs_new, pattern)


def solution(mesh):
    split_rows = ("lat", "lon")
    in_specs = (
        P(split_rows, None, None, None, None),
        P(split_rows, None, None, None, None),
        P(split_rows, None, None),
        P(),
        P(),
        P(),
        P(),
    )
    out_specs = (P(split_rows, None, None, None, None), P(split_rows, None, None))
    return jax.shard_map(local, mesh=mesh, in_specs=in_specs, out_specs=out_specs, check_vma=False)
```

profile of v0, /device:TPU:0, one launch (start us, length us, event | category | flops | bytes accessed | tf_op | source)
XLA Modules:
  0.0 230.0 jit_solution(12648829552232388088)
XLA Ops:
  0.6 12.5 %copy.33.old_ref = f32[20,2,3,50,640]{4,3,2,1,0:T(8,128)} copy(f32[20,2,3,50,640]{4,1,3,2,0:T(2,128)} %param.7) | data formatting | bytes 30720000 | tf_op args[0]
  13.2 0.0 copy-start.3
  13.2 0.0 copy-start.2
  13.2 0.0 copy-start.1
  13.2 7.8 %copy.34.noise_ref = bf16[20,2,3,50,640]{4,3,2,1,0:T(8,128)(2,1)} copy(bf16[20,2,3,50,640]{4,1,3,2,0:T(2,128)(2,1)} %param.8) | data formatting | bytes 15360000 | tf_op args[1]
  21.0 0.0 copy-done.3
  21.0 0.0 copy-done.2
  21.0 0.6 dynamic_slice.3.waves_ref
  21.6 0.0 copy-done.1
  21.6 0.1 broadcast_multiply_fusion
  21.7 0.6 pad.4.spread_ref
  22.3 54.9 %shard_map.86 = (f32[20,2,3,50,640]{4,3,2,1,0:T(8,128)}, f32[5,32,8,1024]{3,2,1,0:T(8,128)}) custom-call(s32[640]{0:T(1024)} %order_ref.1, s32[20]{0:T(128)} %dynamic_slice.3.waves_ref, f32[3]{0:T(128)} %decay_ref.1, f32[20,2,3,50,640]{4,3,2,1,0:T(8,128)} %copy.33.old_ref, bf16[20,2,3,50,640]{4,3,2,1,0:T(8,128)(2,1)} %copy.34.noise_ref, ...), custom_call_target="tpu_custom_call" | custom-call | tf_op jit(solution)/shard_map/pallas_call | solution.py:115
  77.2 5.6 %copy.35 = f32[5,32,8,1024]{3,2,0,1:T(8,128)} copy(f32[5,32,8,1024]{3,2,1,0:T(8,128)} %get-tuple-element.5) | data formatting | bytes 10485760 | tf_op jit(solution)/shard_map/pallas_call | solution.py:115
  82.9 7.6 %all-to-all-start = ((f32[5,32,8,1024]{3,2,0,1:T(8,128)}), f32[5,32,8,1024]{3,2,0,1:T(8,128)}, u32[]{:S(2)}, u32[]{:S(2)}) async-start(f32[5,32,8,1024]{3,2,0,1:T(8,128)} %copy.35), calls=%async_computation | async-start | bytes 10485760 | tf_op jit(solution)/shard_map/all_to_all | solution.py:145
  90.5 0.1 reshape.169
  90.6 0.1 reshape.170
  90.8 14.0 %cosine_multiply_fusion = (f32[640,1,1280]{2,0,1:T(8,128)S(1)}, f32[640,1,1280]{2,0,1:T(8,128)S(1)}) fusion(s32[640]{0:T(1024)S(1)} %reshape.170, f32[640]{0:T(1024)S(1)} %get-tuple-element.20, f32[640]{0:T(1024)S(1)} %get-tuple-element.21), kind=kLoop, calls=%fused_computation.7 | loop fusion | flops 9011200 | bytes 6561280 | tf_op jit(solution)/shard_map/mul | solution.py:131
  104.7 3.2 %pad_maximum_fusion = f32[640,2,1280]{2,0,1:T(8,128)} fusion(f32[640,1,1280]{2,0,1:T(8,128)S(1)} %get-tuple-element.19, f32[640,1,1280]{2,0,1:T(8,128)S(1)} %get-tuple-element.18), kind=kLoop, calls=%fused_computation | loop fusion | flops 1638400 | bytes 13107200 | tf_op jit(solution)/shard_map/stack | solution.py:131
  108.0 10.7 %copy.38 = f32[640,2,1280]{2,1,0:T(2,128)} copy(f32[640,2,1280]{2,0,1:T(8,128)} %pad_maximum_fusion) | data formatting | bytes 13107200 | tf_op jit(solution)/shard_map/stack | solution.py:131
  118.6 8.7 %reshape.171 = f32[1280,1280]{1,0:T(8,128)} reshape(f32[640,2,1280]{2,1,0:T(2,128)} %copy.38) | data formatting | bytes 13107200 | tf_op jit(solution)/shard_map/reshape | solution.py:131
  127.3 22.6 %copy.39 = f32[20,2,3,50,640]{4,1,3,2,0:T(2,128)} copy(f32[20,2,3,50,640]{4,3,2,1,0:T(8,128)} %get-tuple-element.16) | data formatting | bytes 30720000
  149.9 54.8 %all-to-all-done = f32[5,32,8,1024]{3,2,0,1:T(8,128)} async-done(((f32[5,32,8,1024]{3,2,0,1:T(8,128)}), f32[5,32,8,1024]{3,2,0,1:T(8,128)}, u32[]{:S(2)}, u32[]{:S(2)}) %all-to-all-start) | async-done | bytes 5242912 | tf_op jit(solution)/shard_map/all_to_all | solution.py:145
  204.7 0.0 copy-start
  204.7 3.3 %copy.36 = f32[5,32,8,1024]{3,2,1,0:T(8,128)S(1)} copy(f32[5,32,8,1024]{3,2,0,1:T(8,128)} %all-to-all-done) | data formatting | bytes 10485760 | tf_op jit(solution)/shard_map/all_to_all | solution.py:145
  208.0 1.1 copy-done
  209.1 14.2 %fusion = f32[1000,1280]{1,0:T(8,128)} fusion(f32[1280,1280]{1,0:T(8,128)S(1)} %copy-done, f32[1280,1024]{1,0:T(8,128)S(1)} %bitcast.3), kind=kOutput, calls=%fused_computation.1 | convolution fusion | flops 9830400000 | bytes 16916480 | tf_op jit(solution)/shard_map/dot_general | solution.py:149
  223.4 6.6 %reshape.172 = f32[20,50,1280]{2,1,0:T(8,128)} reshape(f32[1000,1280]{1,0:T(8,128)} %fusion) | data formatting | bytes 10240000 | tf_op jit(solution)/shard_map/reshape | solution.py:150
  (3 shorter events, 0.0 us)
Async XLA Ops:
  13.2 7.8 %copy-start.3 = (f32[3]{0:T(128)S(1)}, f32[3]{0:T(128)}, u32[]{:S(2)}) copy-start(f32[3]{0:T(128)} %decay_ref.1) | copy-start | bytes 40
  13.2 7.8 %copy-start.2 = (s32[640]{0:T(1024)S(1)}, s32[640]{0:T(1024)}, u32[]{:S(2)}) copy-start(s32[640]{0:T(1024)} %param.12) | copy-start | bytes 7684
  13.2 8.5 %copy-start.1 = (f32[3,640]{1,0:T(4,128)S(1)}, f32[3,640]{1,0:T(4,128)}, u32[]{:S(2)}) copy-start(f32[3,640]{1,0:T(4,128)} %param.11) | copy-start | bytes 23044
  82.9 121.8 %all-to-all-start = ((f32[5,32,8,1024]{3,2,0,1:T(8,128)}), f32[5,32,8,1024]{3,2,0,1:T(8,128)}, u32[]{:S(2)}, u32[]{:S(2)}) async-start(f32[5,32,8,1024]{3,2,0,1:T(8,128)} %copy.35), calls=%async_computation | async-start | bytes 10485760 | tf_op jit(solution)/shard_map/all_to_all | solution.py:145
  204.7 4.4 %copy-start = (f32[1280,1280]{1,0:T(8,128)S(1)}, f32[1280,1280]{1,0:T(8,128)}, u32[]{:S(2)}) copy-start(f32[1280,1280]{1,0:T(8,128)} %reshape.171) | copy-start | bytes 19660804
where the time goes:
time: 233 us; the launch traced here: 230 us
  local copies, waits for them, and re-layouts  80.4 us (35%)
  Pallas kernels  54.9 us (24%)
  waiting for transfers between devices  54.8 us (24%)
  other arithmetic  17.3 us (7%)
  matrix products  14.2 us (6%)
  starting transfers between devices  7.62 us (3%)
    pallas_call x1, Pallas kernels, transform(): pl.pallas_call(transform_kernel, grid_spec=spec, out_shape=[jax.ShapeDtyp...  54.9 us
    all_to_all x1, waiting for transfers between devices, local(): lax.all_to_all(send, ('lat', 'lon'), split_axis=1, concat_axis=1, tiled=T...  54.8 us
    unnamed x11, local copies, waits for them, and re-layouts  44 us
    dot_general x1, matrix products, local(): lax.dot_general(values, table, (((0,), (0,)), ((), ())), precision=lax.Pr...  14.2 us
    mul x1, other arithmetic, synthesis_table(): weight * jnp.cos(angle)  14 us
    another operation x1, local copies, waits for them, and re-layouts, synthesis_table(): jnp.stack([weight * jnp.cos(angle), -weight * jnp.sin(angle)], axis=1)  10.7 us
    reshape x1, local copies, waits for them, and re-layouts, synthesis_table(): jnp.stack([weight * jnp.cos(angle), -weight * jnp.sin(angle)], axis=1)  8.66 us
    all_to_all x1, starting transfers between devices, local(): lax.all_to_all(send, ('lat', 'lon'), split_axis=1, concat_axis=1, tiled=T...  7.62 us
  transfers between devices with their start and end apart: 1, of which 1 were waited for; matrix products, arithmetic and copies ran while one was open for 26% of the time, Pallas kernels for 0%

commit v1 on v0

v1 whole, which is shorter than its diff:
```python
import functools

import jax
import jax.numpy as jnp
from jax import lax
from jax.experimental import pallas as pl
from jax.experimental.pallas import tpu as pltpu
from jax.sharding import PartitionSpec as P

TWO_PI = 6.283185307179586
LANES = 128
HALF = 64
MESH = pl.DeviceIdType.MESH


def round_up(size, unit):
    return -(-size // unit) * unit


def group_size(slots):
    return 4 if slots % 4 == 0 else slots


def split(x):
    high = x.astype(jnp.bfloat16)
    return high, (x - high.astype(jnp.float32)).astype(jnp.bfloat16)


def legendre_product(basis, both):
    contract = (((1,), (1,)), ((), ()))
    basis_high, basis_low = split(basis)
    first = lax.dot_general(basis_high, both, contract, preferred_element_type=jnp.float32)
    second = lax.dot_general(basis_low, both[:LANES], contract, preferred_element_type=jnp.float32)
    return first[:, :LANES] + first[:, LANES:] + second


def pack_group(order_ref, field, store, devices, lat_dev, members, rows, wide):
    lane = lax.broadcasted_iota(jnp.int32, (rows, LANES), 1)

    def pack(device, carry):
        tiles = [jnp.zeros((rows, LANES), jnp.float32) for _ in range(wide // LANES)]
        for q in range(lat_dev):
            piece = field[order_ref[device * lat_dev + q]]
            start = members * q
            offset = start % LANES
            if offset:
                piece = pltpu.roll(piece, offset, axis=1)
            tile = start // LANES
            tiles[tile] = jnp.where((lane >= offset) & (lane < offset + members), piece, tiles[tile])
            if offset + members > LANES:
                tiles[tile + 1] = jnp.where(lane < offset + members - LANES, piece, tiles[tile + 1])
        for index, tile in enumerate(tiles):
            store(device, index, tile)
        return carry

    lax.fori_loop(0, devices, pack, 0)


def update_kernel(group, order_ref, waves_ref, decay_ref, old_ref, noise_ref, basis_ref, spread_ref, new_ref, both_ref, send_ref, weights, field):
    step = pl.program_id(0)
    scales, members, parts, width = old_ref.shape[1:]
    devices, rows, wide = send_ref.shape
    lat_dev = order_ref.shape[0] // devices

    @pl.when(step == 0)
    def _():
        weights[...] = jnp.zeros_like(weights)
        if 2 * group < rows:
            field[...] = jnp.zeros_like(field)

    wave = waves_ref[step]
    live = lax.broadcasted_iota(jnp.int32, (8, width), 1) + wave < width
    shifted = jnp.where(live, pltpu.roll(spread_ref[...], width - wave, axis=1), 0.0)
    total = None
    for scale in range(scales):
        keep = jnp.where(live[:1], decay_ref[scale], 0.0).reshape(1, 1, width)
        fresh = shifted[scale : scale + 1, :].reshape(1, 1, width)
        value = keep * old_ref[0, scale] + fresh * noise_ref[0, scale].astype(jnp.float32)
        new_ref[0, scale] = value
        total = value if total is None else total + value
    for part in range(parts):
        weights[part * HALF : part * HALF + members, :] = total[:, part, :]
    high, low = split(weights[...])
    both_ref[0, :LANES] = high
    both_ref[0, LANES:] = low

    @pl.when(step < group)
    def _():
        product = legendre_product(basis_ref[0], both_ref[0])
        other = pltpu.roll(product, HALF, axis=1)
        for index in range(group):

            @pl.when(step == index)
            def _(index=index):
                field[:, 2 * index, :] = product
                field[:, 2 * index + 1, :] = other

    @pl.when(step == group - 1)
    def _():
        def store(device, index, tile):
            send_ref[device, :, index * LANES : (index + 1) * LANES] = tile

        pack_group(order_ref, field, store, devices, lat_dev, members, rows, wide)


def update(old, noise, legendre, spread, decay, waves, lat_order, devices, rows, wide, group):
    slots, scales, members, parts, width = old.shape
    lats = legendre.shape[1]

    def slot5(i, *_):
        return (i, 0, 0, 0, 0)

    spec = pltpu.PrefetchScalarGridSpec(
        num_scalar_prefetch=3,
        grid=(slots,),
        in_specs=[
            pl.BlockSpec((1, scales, members, parts, width), slot5),
            pl.BlockSpec((1, scales, members, parts, width), slot5),
            pl.BlockSpec((1, lats, width), lambda i, *_: (jnp.minimum(i, group - 1), 0, 0)),
            pl.BlockSpec((8, width), lambda i, *_: (0, 0)),
        ],
        out_specs=[
            pl.BlockSpec((1, scales, members, parts, width), slot5),
            pl.BlockSpec((1, 2 * LANES, width), lambda i, *_: (i, 0, 0)),
            pl.BlockSpec((devices, rows, wide), lambda i, *_: (0, 0, 0)),
        ],
        scratch_shapes=[
            pltpu.VMEM((LANES, width), jnp.float32),
            pltpu.VMEM((lats, rows, LANES), jnp.float32),
        ],
    )
    return pl.pallas_call(
        functools.partial(update_kernel, group),
        grid_spec=spec,
        out_shape=[
            jax.ShapeDtypeStruct(old.shape, jnp.float32),
            jax.ShapeDtypeStruct((slots, 2 * LANES, width), jnp.bfloat16),
            jax.ShapeDtypeStruct((devices, rows, wide), jnp.float32),
        ],
        compiler_params=pltpu.CompilerParams(dimension_semantics=("arbitrary",)),
        name="update",
    )(lat_order, waves, decay, old, noise, legendre, spread)


def exchange_kernel(
    group, members, order_ref, first_ref, both_hbm, basis_hbm, phase_ref, out_ref,
    basis, both, field, send, recv, turned, left, table, load_sem, own_sem, send_sem, recv_sem,
):
    lat_size, lon_size = lax.axis_size("lat"), lax.axis_size("lon")
    devices = lat_size * lon_size
    me = lax.axis_index("lat") * lon_size + lax.axis_index("lon")
    slots, lats = basis_hbm.shape[0], basis_hbm.shape[1]
    groups, _, rows, wide = recv.shape
    lat_dev = lats // devices
    padded, length = out_ref.shape[1], out_ref.shape[2]
    depth = devices * rows

    def peer(k):
        other = lax.rem(me + k, devices)
        return other, (other // lon_size, lax.rem(other, lon_size))

    barrier = pltpu.get_barrier_semaphore()

    def greet(k, carry):
        pl.semaphore_signal(barrier, inc=1, device_id=peer(k)[1], device_id_type=MESH)
        return carry

    lax.fori_loop(1, devices, greet, 0)

    def loads(slot):
        side = lax.rem(slot, 2)
        return (
            pltpu.make_async_copy(basis_hbm.at[slot], basis.at[side], load_sem.at[0, side]),
            pltpu.make_async_copy(both_hbm.at[slot], both.at[side], load_sem.at[1, side]),
        )

    if slots > group:
        for copy in loads(group):
            copy.start()
    left[...] = jnp.zeros_like(left)
    if 2 * group < rows:
        field[...] = jnp.zeros_like(field)
    pl.semaphore_wait(barrier, devices - 1)

    def send_group(source, index):
        def one(k, carry):
            other, where = peer(k)
            pltpu.make_async_remote_copy(
                src_ref=source.at[other],
                dst_ref=recv.at[index, me],
                send_sem=send_sem.at[index],
                recv_sem=recv_sem.at[index],
                device_id=where,
                device_id_type=MESH,
            ).start()
            return carry

        lax.fori_loop(1, devices, one, 0)
        pltpu.make_async_copy(source.at[me], recv.at[index, me], own_sem.at[index]).start()

    send_group(first_ref, 0)

    def transform(index, carry):
        for inner in range(group):
            slot = index * group + inner
            for copy in loads(slot):
                copy.wait()

            @pl.when(slot + 1 < slots)
            def _():
                for copy in loads(slot + 1):
                    copy.start()

            side = lax.rem(slot, 2)
            product = legendre_product(basis[side], both[side])
            field[:, 2 * inner, :] = product
            field[:, 2 * inner + 1, :] = pltpu.roll(product, HALF, axis=1)

        def store(device, tile_index, tile):
            send[index - 1, device, :, tile_index * LANES : (tile_index + 1) * LANES] = tile

        pack_group(order_ref, field, store, devices, lat_dev, members, rows, wide)
        send_group(send.at[index - 1], index)
        return carry

    lax.fori_loop(1, groups, transform, 0)

    def make_table(index):
        wave = phase_ref[pl.ds(pl.multiple_of(index * depth, depth), depth), :]
        lane = lax.broadcasted_iota(jnp.int32, wave.shape, 1).astype(jnp.float32)
        row = lax.broadcasted_iota(jnp.int32, wave.shape, 0)
        quarter = jnp.where(lax.rem(row, 2) == 0, 0.0, TWO_PI / 4)
        weight = jnp.where(wave == 0.0, 1.0, 2.0)

        def angle(steps):
            turns = jnp.floor(steps * (1.0 / length))
            return (steps - turns * length) * (TWO_PI / length)

        base = angle(wave * lane) + quarter
        cosine, sine = weight * jnp.cos(base), weight * jnp.sin(base)
        for block in range(length // LANES):
            if block == 0:
                value = cosine
            else:
                value = jnp.cos(angle(wave * float(LANES * block))) * cosine - jnp.sin(angle(wave * float(LANES * block))) * sine
            high, low = split(value)
            span = slice(block * LANES, (block + 1) * LANES)
            table[:depth, span] = high
            table[depth : 2 * depth, span] = high
            table[2 * depth :, span] = low

    def synthesis(index, carry):
        make_table(index)
        pltpu.make_async_copy(recv.at[index, pl.ds(0, devices - 1)], recv.at[index, pl.ds(0, devices - 1)], recv_sem.at[index]).wait()
        pltpu.make_async_copy(recv.at[index, 0], recv.at[index, 0], own_sem.at[index]).wait()
        turned[...] = recv[index].reshape(depth, wide).T
        for q in range(lat_dev):
            high, low = split(turned[members * q : members * (q + 1), :])
            left[q, :members, :depth] = high.astype(jnp.float32)
            left[q, :members, depth:] = low.astype(jnp.float32)
        values = left[...].reshape(lat_dev * padded, 2 * depth).astype(jnp.bfloat16)
        chunk = 2 * LANES

        def columns(n, carry):
            span = pl.ds(pl.multiple_of(n * chunk, chunk), chunk)
            part = jnp.dot(values, table[: 2 * depth, span], preferred_element_type=jnp.float32)
            part += jnp.dot(values[:, :depth], table[2 * depth :, span], preferred_element_type=jnp.float32)
            part = part.reshape(lat_dev, padded, chunk)

            @pl.when(index == 0)
            def _():
                out_ref[:, :, span] = part

            @pl.when(index > 0)
            def _():
                out_ref[:, :, span] += part

            return carry

        lax.fori_loop(0, length // chunk, columns, 0)
        return carry

    lax.fori_loop(0, groups, synthesis, 0)

    def sent(index, carry):
        pltpu.make_async_copy(recv.at[index, pl.ds(0, devices - 1)], recv.at[index, pl.ds(0, devices - 1)], send_sem.at[index]).wait()
        return carry

    lax.fori_loop(0, groups, sent, 0)


def exchange(first, both, legendre, phase, lat_order, members, group, length):
    devices, rows, wide = first.shape
    slots, lats, width = legendre.shape
    groups = slots // group
    lat_dev = lats // devices
    padded = round_up(members, 8)
    depth = devices * rows
    anywhere = pl.BlockSpec(memory_space=pl.ANY)
    return pl.pallas_call(
        functools.partial(exchange_kernel, group, members),
        in_specs=[
            pl.BlockSpec(memory_space=pltpu.SMEM),
            anywhere,
            anywhere,
            anywhere,
            pl.BlockSpec(memory_space=pltpu.VMEM),
        ],
        out_specs=pl.BlockSpec(memory_space=pltpu.VMEM),
        out_shape=jax.ShapeDtypeStruct((lat_dev, padded, length), jnp.float32),
        scratch_shapes=[
            pltpu.VMEM((2, lats, width), jnp.float32),
            pltpu.VMEM((2, 2 * LANES, width), jnp.bfloat16),
            pltpu.VMEM((lats, rows, LANES), jnp.float32),
            pltpu.VMEM((max(groups - 1, 1), devices, rows, wide), jnp.float32),
            pltpu.VMEM((groups, devices, rows, wide), jnp.float32),
            pltpu.VMEM((wide, depth), jnp.float32),
            pltpu.VMEM((lat_dev, padded, 2 * depth), jnp.float32),
            pltpu.VMEM((3 * depth, length), jnp.bfloat16),
            pltpu.SemaphoreType.DMA((2, 2)),
            pltpu.SemaphoreType.DMA((groups,)),
            pltpu.SemaphoreType.DMA((groups,)),
            pltpu.SemaphoreType.DMA((groups,)),
        ],
        compiler_params=pltpu.CompilerParams(collective_id=0, has_side_effects=True),
        name="exchange",
    )(lat_order, first, both, legendre, phase)


def local(coeffs_old, noise, legendre, decay, amplitude, wavenumber_of_slot, lat_order):
    devices = lax.axis_size("lat") * lax.axis_size("lon")
    me = lax.axis_index("lat") * lax.axis_size("lon") + lax.axis_index("lon")
    slots, parts, scales, members, width = coeffs_old.shape
    lats = legendre.shape[1]
    length = 2 * lats
    lat_dev = lats // devices
    group = group_size(slots)
    groups = slots // group
    rows = round_up(parts * group, 8)
    wide = round_up(lat_dev * members, LANES)
    mine = lax.dynamic_slice_in_dim(wavenumber_of_slot, me * slots, slots)
    spread = jnp.pad(amplitude * jnp.sqrt(1.0 - decay * decay)[:, None], ((0, 8 - scales), (0, 0)))
    waves = wavenumber_of_slot.astype(jnp.float32).reshape(devices, groups, group).transpose(1, 0, 2)
    waves = jnp.pad(jnp.repeat(waves, parts, axis=2), ((0, 0), (0, 0), (0, rows - parts * group)))
    phase = jnp.broadcast_to(waves.reshape(-1, 1), (groups * devices * rows, LANES))
    turn = (0, 2, 3, 1, 4)
    new, both, first = update(
        coeffs_old.transpose(turn), noise.transpose(turn), legendre, spread, decay, mine, lat_order, devices, rows, wide, group
    )
    coeffs_new = new.transpose(0, 3, 1, 2, 4)
    out = exchange(first, both, legendre, phase, lat_order, members, group, length)
    return (coeffs_new, out[:, :members, :])


def solution(mesh):
    split_rows = ("lat", "lon")
    in_specs = (
        P(split_rows, None, None, None, None),
        P(split_rows, None, None, None, None),
        P(split_rows, None, None),
        P(),
        P(),
        P(),
        P(),
    )
    out_specs = (P(split_rows, None, None, None, None), P(split_rows, None, None))
    return jax.shard_map(local, mesh=mesh, in_specs=in_specs, out_specs=out_specs, check_vma=False)
```

time: 233 us -> 184 us (0.79)
  Pallas kernels: 54.9 us -> 171 us
  local copies, waits for them, and re-layouts: 80.4 us -> 9.19 us
  waiting for transfers between devices: 54.8 us -> 0 us
  other arithmetic: 17.3 us -> 2.13 us
  matrix products: 14.2 us -> 0 us
  starting transfers between devices: 7.62 us -> 0 us
    pallas_call x1 -> x2, Pallas kernels: 54.9 us -> 171 us  [the longest x1 129 us: exchange(): pl.pallas_call(functools.partial(exchange_kernel, group, members), in_spe...]
    all_to_all x1 -> x0, waiting for transfers between devices: 54.8 us -> none  [local(): lax.all_to_all(send, ('lat', 'lon'), split_axis=1, concat_axis=1, tiled=T...]
    unnamed x11 -> x1, local copies, waits for them, and re-layouts: 44 us -> 5.55 us
    reshape x4 -> x1, local copies, waits for them, and re-layouts: 15.5 us -> 0.1 us  [local(): wavenumber_of_slot.astype(jnp.float32).reshape(devices, groups, group)]
    dot_general x1 -> x0, matrix products: 14.2 us -> none  [local(): lax.dot_general(values, table, (((0,), (0,)), ((), ())), precision=lax.Pr...]
    mul x1 -> x0, other arithmetic: 14 us -> none  [synthesis_table(): weight * jnp.cos(angle)]
    another operation x1 -> x0, local copies, waits for them, and re-layouts: 10.7 us -> none  [synthesis_table(): jnp.stack([weight * jnp.cos(angle), -weight * jnp.sin(angle)], axis=1)]
    all_to_all x1 -> x0, starting transfers between devices: 7.62 us -> none  [local(): lax.all_to_all(send, ('lat', 'lon'), split_axis=1, concat_axis=1, tiled=T...]
  transfers between devices with their start and end apart: 1 -> 0, of which waited for: 1 -> 0; matrix products, arithmetic and copies ran while one was open for 26% -> 0% of each run, Pallas kernels for 0% -> 0%
where the time goes in v1:
time: 184 us; the launch traced here: 183 us
  Pallas kernels  171 us (93%)
  local copies, waits for them, and re-layouts  9.19 us (5%)
  other arithmetic  2.13 us (1%)
    pallas_call x1, Pallas kernels, exchange(): pl.pallas_call(functools.partial(exchange_kernel, group, members), in_spe...  129 us
    pallas_call x1, Pallas kernels, update(): pl.pallas_call(functools.partial(update_kernel, group), grid_spec=spec, o...  42.2 us
    unnamed x1, local copies, waits for them, and re-layouts  5.55 us

profile of v1, /device:TPU:0, one launch (start us, length us, event | category | flops | bytes accessed | tf_op | source)
XLA Modules:
  0.0 182.8 jit_solution(11089529730011473304)
XLA Ops:
  0.6 1.3 dynamic_slice.3.waves_ref
  1.9 0.7 subtract_sqrt_fusion
  2.6 0.7 convert_element_type.5
  3.3 0.8 broadcast_multiply_fusion
  4.1 0.6 pad.4.spread_ref
  4.7 0.1 reshape.12
  4.8 0.2 broadcast_in_dim.11
  5.0 0.3 broadcast_in_dim.12
  5.3 1.1 broadcast_in_dim.13.phase_ref
  6.4 42.2 %update.1 = (f32[20,3,50,2,640]{4,3,2,1,0:T(2,128)}, bf16[20,256,640]{2,1,0:T(8,128)(2,1)}, f32[32,8,1024]{2,1,0:T(8,128)}) custom-call(s32[640]{0:T(1024)} %order_ref.3, s32[20]{0:T(128)} %dynamic_slice.3.waves_ref, f32[3]{0:T(128)} %decay_ref.1, f32[20,3,50,2,640]{4,3,2,1,0:T(2,128)} %bitcast.6, bf16[20,3,50,2,640]{4,3,2,1,0:T(2,128)(2,1)} %bitcast.7, ...), custom_call_target="tpu_custom_call" | custom-call | tf_op jit(solution)/shard_map/update/pallas_call | solution.py:132
  48.6 128.6 %exchange.1 = f32[20,56,1280]{2,1,0:T(8,128)} custom-call(s32[640]{0:T(1024)} %order_ref.3, f32[32,8,1024]{2,1,0:T(8,128)} %get-tuple-element.6.first_ref, bf16[20,256,640]{2,1,0:T(8,128)(2,1)} %get-tuple-element.7.both_hbm, f32[20,640,640]{2,1,0:T(8,128)} %basis_hbm.1, f32[1280,128]{1,0:T(8,128)} %broadcast_in_dim.13.phase_ref), custom_call_target="tpu_custom_call" | custom-call | tf_op jit(solution)/shard_map/exchange/pallas_call | solution.py:300
  177.2 5.5 %copy.12 = f32[20,50,1280]{2,1,0:T(8,128)} copy(f32[20,50,1280]{2,1,0:T(8,128)} %bitcast.5) | data formatting | bytes 10240000
  (1 shorter events, 0.0 us)

commit v2 on v0

v2 whole, which is shorter than its diff:
```python
import functools

import jax
import jax.numpy as jnp
from jax import lax
from jax.experimental import pallas as pl
from jax.experimental.pallas import tpu as pltpu
from jax.sharding import PartitionSpec as P

TWO_PI = 6.283185307179586
LANES = 128
SUBLANES = 8
HALF = 64
PARTS = 2
MESH = pl.DeviceIdType.MESH


def round_up(size, unit):
    return -(-size // unit) * unit


def split(x):
    high = x.astype(jnp.bfloat16)
    return high, (x - high.astype(jnp.float32)).astype(jnp.bfloat16)


class Group:
    def __init__(self, size, lat_dev, members):
        used = PARTS * size
        self.size = size
        self.fold = SUBLANES // used if SUBLANES % used == 0 and lat_dev % (SUBLANES // used) == 0 else 1
        self.rows = round_up(self.fold * used, SUBLANES)
        self.padded = self.rows > self.fold * used
        self.lat = lat_dev // self.fold
        self.wide = round_up(self.lat * members, LANES)

    def block(self, devices):
        return (devices, self.rows, self.wide)


def plan(slots, lat_dev, members):
    if slots % 4 == 0 and slots >= 8:
        sizes = (2, 4, slots // 4 - 1, 2)
    elif slots > 4 and slots % 4:
        sizes = (slots % 4, 4, slots // 4 - 1, 4)
    else:
        sizes = (1, 1, slots - 2, 1)
    first, middle, count, last = sizes
    return Group(first, lat_dev, members), Group(middle, lat_dev, members), count, Group(last, lat_dev, members)


def position():
    lat_size, lon_size = lax.axis_size("lat"), lax.axis_size("lon")
    return lax.axis_index("lat") * lon_size + lax.axis_index("lon"), lat_size * lon_size, lon_size


def gains_kernel(waves_ref, decay_ref, amplitude_ref, gains_ref):
    slots, _, width = gains_ref.shape
    scales = amplitude_ref.shape[0]
    me = position()[0]
    row = lax.broadcasted_iota(jnp.int32, (SUBLANES, width), 0)
    column = lax.broadcasted_iota(jnp.int32, (SUBLANES, width), 1)
    table = jnp.zeros((SUBLANES, width), jnp.float32)
    for scale in range(scales):
        decay = jnp.full((1, width), decay_ref[scale], jnp.float32)
        table = jnp.where(row == scale, amplitude_ref[scale : scale + 1, :] * jnp.sqrt(1.0 - decay * decay), table)
        table = jnp.where(row == scales + scale, decay, table)

    def one(slot, carry):
        wave = waves_ref[me * slots + slot]
        gains_ref[slot] = jnp.where(column + wave < width, pltpu.roll(table, width - wave, axis=1), 0.0)
        return carry

    lax.fori_loop(0, slots, one, 0)


def gains_of_slots(waves, decay, amplitude, slots):
    smem = pl.BlockSpec(memory_space=pltpu.SMEM)
    vmem = pl.BlockSpec(memory_space=pltpu.VMEM)
    return pl.pallas_call(
        gains_kernel,
        in_specs=[smem, smem, vmem],
        out_specs=vmem,
        out_shape=jax.ShapeDtypeStruct((slots, SUBLANES, amplitude.shape[1]), jnp.float32),
        name="gains",
    )(waves, decay, amplitude)


def turn_block(block_ref, group, turned, left, lat_dev, members):
    devices, rows, wide = block_ref.shape
    depth = devices * rows
    turned[:wide, :depth] = block_ref[...].reshape(depth, wide).T
    column = lax.broadcasted_iota(jnp.int32, (1, depth), 1)
    fold = lax.rem(column // (PARTS * group.size), group.fold)
    for q in range(lat_dev):
        start = members * (q % group.lat)
        piece = turned[start : start + members, :depth]
        if group.fold > 1:
            piece = jnp.where(fold == q // group.lat, piece, 0.0)
        high, low = split(piece)
        left[q, :members, :depth] = high.astype(jnp.float32)
        left[q, :members, depth : 2 * depth] = low.astype(jnp.float32)


def contract(values, table, depth):
    both = jnp.dot(values, table[: 2 * depth], preferred_element_type=jnp.float32)
    return both + jnp.dot(values[:, :depth], table[2 * depth :], preferred_element_type=jnp.float32)


def exchange_kernel(
    first, middle, count, last, members,
    order_ref, waves_ref, gains_ref, old_hbm, noise_hbm, basis_hbm,
    sum_hbm, arrived_hbm, table_hbm,
    old, noise, basis, weights, field, send_first, send_middle, send_last, recv_first, recv_middle,
    wave, turned, left, table, total, load_sem, own_sem, send_sem, recv_sem, out_sem,
):
    me, devices, lon_size = position()
    slots, lats, width = basis_hbm.shape
    scales = old_hbm.shape[1]
    lat_dev, padded, length = total.shape
    final = count + 1

    def peer(other):
        return other // lon_size, lax.rem(other, lon_size)

    barrier = pltpu.get_barrier_semaphore()

    def greet(k, carry):
        pl.semaphore_signal(barrier, inc=1, device_id=peer(lax.rem(me + k, devices)), device_id_type=MESH)
        return carry

    lax.fori_loop(1, devices, greet, 0)

    def loads(slot):
        side = lax.rem(slot, 2)
        return (
            pltpu.make_async_copy(old_hbm.at[slot], old.at[side], load_sem.at[0, side]),
            pltpu.make_async_copy(noise_hbm.at[slot], noise.at[side], load_sem.at[1, side]),
            pltpu.make_async_copy(basis_hbm.at[slot], basis.at[side], load_sem.at[2, side]),
        )

    for copy in loads(0):
        copy.start()
    weights[...] = jnp.zeros_like(weights)
    if first.padded or middle.padded or last.padded:
        field[...] = jnp.zeros_like(field)

    def transform(group, start):
        for inner in range(group.size):
            slot = start + inner

            @pl.when(slot + 1 < slots)
            def _():
                for copy in loads(slot + 1):
                    copy.start()

            for copy in loads(slot):
                copy.wait()
            side = lax.rem(slot, 2)
            summed = None
            for scale in range(scales):
                fresh = gains_ref[slot, scale : scale + 1, :].reshape(1, 1, width)
                keep = gains_ref[slot, scales + scale : scales + scale + 1, :].reshape(1, 1, width)
                value = keep * old[side, scale] + fresh * noise[side, scale].astype(jnp.float32)
                summed = value if summed is None else summed + value
            for part in range(PARTS):
                weights[part * HALF : part * HALF + members, :] = summed[:, part, :]
            high, low = split(weights[...])
            basis_high, basis_low = split(basis[side])
            lanes = (((1,), (1,)), ((), ()))
            pair = lax.dot_general(basis_high, jnp.concatenate([high, low], axis=0), lanes, preferred_element_type=jnp.float32)
            small = lax.dot_general(basis_low, high, lanes, preferred_element_type=jnp.float32)
            product = pair[:, :LANES] + pair[:, LANES:] + small
            other = pltpu.roll(product, HALF, axis=1)
            for fold in range(group.fold):
                row = PARTS * (fold * group.size + inner)
                field[:, row, :] = product
                field[:, row + 1, :] = other

    def pack_and_send(group, send, recv, index):
        rows = group.rows
        lane = lax.broadcasted_iota(jnp.int32, (rows, LANES), 1)
        fold = lax.broadcasted_iota(jnp.int32, (rows, LANES), 0) // (PARTS * group.size)

        def remote(other):
            return pltpu.make_async_remote_copy(
                src_ref=send.at[other],
                dst_ref=recv.at[me],
                send_sem=send_sem.at[index],
                recv_sem=recv_sem.at[index],
                device_id=peer(other),
                device_id_type=MESH,
            )

        def one(k, carry):
            other = lax.rem(me + k, devices)
            tiles = [jnp.zeros((rows, LANES), jnp.float32) for _ in range(group.wide // LANES)]
            for q in range(lat_dev):
                piece = field[order_ref[other * lat_dev + q]][:rows]
                start = members * (q % group.lat)
                offset = start % LANES
                if offset:
                    piece = pltpu.roll(piece, offset, axis=1)
                tile = start // LANES
                keep = (lane >= offset) & (lane < offset + members)
                spill = lane < offset + members - LANES
                if group.fold > 1:
                    keep &= fold == q // group.lat
                    spill &= fold == q // group.lat
                tiles[tile] = jnp.where(keep, piece, tiles[tile])
                if offset + members > LANES:
                    tiles[tile + 1] = jnp.where(spill, piece, tiles[tile + 1])
            for position_, value in enumerate(tiles):
                send[other, :, position_ * LANES : (position_ + 1) * LANES] = value

            @pl.when(k == 1)
            def _():
                pltpu.make_async_copy(send.at[me], recv.at[me], own_sem.at[index]).start()

            @pl.when(k > 1)
            def _():
                remote(lax.rem(me + k - 1, devices)).start()

            return carry

        lax.fori_loop(0, devices, one, 0)
        remote(lax.rem(me + devices - 1, devices)).start()

    def await_group(recv, index):
        others = recv.at[pl.ds(0, devices - 1)]
        pltpu.make_async_copy(others, others, recv_sem.at[index]).wait()
        pltpu.make_async_copy(recv.at[0], recv.at[0], own_sem.at[index]).wait()

    transform(first, 0)
    pl.semaphore_wait(barrier, devices - 1)
    pack_and_send(first, send_first, recv_first, 0)

    def middle_step(step, carry):
        transform(middle, first.size + step * middle.size)
        pack_and_send(middle, send_middle.at[step], recv_middle.at[step], step + 1)
        return carry

    lax.fori_loop(0, count, middle_step, 0)
    transform(last, slots - last.size)
    pack_and_send(last, send_last, arrived_hbm, final)

    def make_table(group, start):
        rows = group.rows
        depth = devices * rows
        slot = lax.rem(lax.broadcasted_iota(jnp.int32, (rows, LANES), 0) // PARTS, group.size)

        def fill(device, carry):
            tile = jnp.zeros((rows, LANES), jnp.int32)
            for inner in range(group.size):
                tile = jnp.where(slot == inner, waves_ref[device * slots + start + inner], tile)
            wave[pl.ds(pl.multiple_of(device * rows, SUBLANES), rows), :] = tile.astype(jnp.float32)
            return carry

        lax.fori_loop(0, devices, fill, 0)
        waves = wave[:depth, :]
        lane = lax.broadcasted_iota(jnp.int32, (depth, LANES), 1).astype(jnp.float32)
        row = lax.broadcasted_iota(jnp.int32, (depth, LANES), 0)

        def angle(steps):
            turns = jnp.floor(steps * (1.0 / length))
            return (steps - turns * length) * (TWO_PI / length)

        base = angle(waves * lane) + jnp.where(lax.rem(row, PARTS) == 0, 0.0, TWO_PI / 4)
        weight = jnp.where(waves == 0.0, 1.0, 2.0)
        cosine, sine = weight * jnp.cos(base), weight * jnp.sin(base)
        stride = angle(waves * float(LANES))
        step_cosine, step_sine = jnp.cos(stride), jnp.sin(stride)
        for block in range(length // LANES):
            if block:
                cosine, sine = cosine * step_cosine - sine * step_sine, sine * step_cosine + cosine * step_sine
            high, low = split(cosine)
            span = slice(block * LANES, (block + 1) * LANES)
            table[:depth, span] = high
            table[depth : 2 * depth, span] = high
            table[2 * depth : 3 * depth, span] = low

    def synthesis(group, recv, index, start, fresh):
        depth = devices * group.rows
        make_table(group, start)
        await_group(recv, index)
        turn_block(recv, group, turned, left, lat_dev, members)
        values = left[:, :, : 2 * depth].reshape(lat_dev * padded, 2 * depth).astype(jnp.bfloat16)
        chunk = 2 * LANES

        def columns(n, carry):
            span = pl.ds(pl.multiple_of(n * chunk, chunk), chunk)
            part = contract(values, table[: 3 * depth, span], depth).reshape(lat_dev, padded, chunk)
            total[:, :, span] = part if fresh else total[:, :, span] + part
            return carry

        lax.fori_loop(0, length // chunk, columns, 0)

    left[...] = jnp.zeros_like(left)
    synthesis(first, recv_first, 0, 0, True)

    def middle_synthesis(step, carry):
        synthesis(middle, recv_middle.at[step], step + 1, first.size + step * middle.size, False)
        return carry

    lax.fori_loop(0, count, middle_synthesis, 0)
    sum_out = pltpu.make_async_copy(total, sum_hbm, out_sem.at[0])
    sum_out.start()
    make_table(last, slots - last.size)
    table_out = pltpu.make_async_copy(table.at[: table_hbm.shape[0]], table_hbm, out_sem.at[1])
    table_out.start()

    def sent(block, index):
        others = block.at[pl.ds(0, devices - 1)]
        pltpu.make_async_copy(others, others, send_sem.at[index]).wait()

    sent(send_first, 0)

    def middle_sent(step, carry):
        sent(send_middle.at[step], step + 1)
        return carry

    lax.fori_loop(0, count, middle_sent, 0)
    sum_out.wait()
    table_out.wait()
    sent(send_last, final)
    await_group(arrived_hbm, final)


def exchange(gains, old, noise, legendre, waves, lat_order, length):
    devices = lax.axis_size("lat") * lax.axis_size("lon")
    slots, scales, members, parts, width = old.shape
    lats = legendre.shape[1]
    lat_dev = lats // devices
    first, middle, count, last = plan(slots, lat_dev, members)
    groups = (first, middle, last)
    padded = round_up(members, SUBLANES)
    depth = devices * max(group.rows for group in groups)
    rows = max(group.rows for group in groups)
    some = max(count, 1)
    smem = pl.BlockSpec(memory_space=pltpu.SMEM)
    anywhere = pl.BlockSpec(memory_space=pl.ANY)
    return pl.pallas_call(
        functools.partial(exchange_kernel, first, middle, count, last, members),
        in_specs=[smem, smem, pl.BlockSpec(memory_space=pltpu.VMEM), anywhere, anywhere, anywhere],
        out_specs=[anywhere, anywhere, anywhere],
        out_shape=[
            jax.ShapeDtypeStruct((lat_dev, padded, length), jnp.float32),
            jax.ShapeDtypeStruct(last.block(devices), jnp.float32),
            jax.ShapeDtypeStruct((3 * devices * last.rows, length), jnp.bfloat16),
        ],
        scratch_shapes=[
            pltpu.VMEM((2, scales, members, parts, width), jnp.float32),
            pltpu.VMEM((2, scales, members, parts, width), jnp.bfloat16),
            pltpu.VMEM((2, lats, width), jnp.float32),
            pltpu.VMEM((LANES, width), jnp.float32),
            pltpu.VMEM((lats, rows, LANES), jnp.float32),
            pltpu.VMEM(first.block(devices), jnp.float32),
            pltpu.VMEM((some,) + middle.block(devices), jnp.float32),
            pltpu.VMEM(last.block(devices), jnp.float32),
            pltpu.VMEM(first.block(devices), jnp.float32),
            pltpu.VMEM((some,) + middle.block(devices), jnp.float32),
            pltpu.VMEM((depth, LANES), jnp.float32),
            pltpu.VMEM((max(group.wide for group in groups), depth), jnp.float32),
            pltpu.VMEM((lat_dev, padded, 2 * depth), jnp.float32),
            pltpu.VMEM((3 * depth, length), jnp.bfloat16),
            pltpu.VMEM((lat_dev, padded, length), jnp.float32),
            pltpu.SemaphoreType.DMA((3, 2)),
            pltpu.SemaphoreType.DMA((count + 2,)),
            pltpu.SemaphoreType.DMA((count + 2,)),
            pltpu.SemaphoreType.DMA((count + 2,)),
            pltpu.SemaphoreType.DMA((2,)),
        ],
        compiler_params=pltpu.CompilerParams(collective_id=0, has_side_effects=True),
        name="exchange",
    )(lat_order, waves, gains, old, noise, legendre)


def finish_kernel(group, members, sum_ref, arrived_ref, table_ref, out_ref, turned, left):
    lat_dev, padded, chunk = sum_ref.shape
    depth = left.shape[2] // 2

    @pl.when(pl.program_id(0) == 0)
    def _():
        left[...] = jnp.zeros_like(left)
        turn_block(arrived_ref, group, turned, left, lat_dev, members)

    values = left[...].reshape(lat_dev * padded, 2 * depth).astype(jnp.bfloat16)
    part = sum_ref[...] + contract(values, table_ref[...], depth).reshape(lat_dev, padded, chunk)
    out_ref[...] = part[:, :members, :]


def finish(summed, arrived, table, slots, members):
    lat_dev, padded, length = summed.shape
    group = plan(slots, lat_dev, members)[3]
    devices, rows, wide = arrived.shape
    depth = devices * rows
    chunk = 2 * LANES
    return pl.pallas_call(
        functools.partial(finish_kernel, group, members),
        grid=(length // chunk,),
        in_specs=[
            pl.BlockSpec((lat_dev, padded, chunk), lambda n: (0, 0, n)),
            pl.BlockSpec((devices, rows, wide), lambda n: (0, 0, 0)),
            pl.BlockSpec((3 * depth, chunk), lambda n: (0, n)),
        ],
        out_specs=pl.BlockSpec((lat_dev, members, chunk), lambda n: (0, 0, n)),
        out_shape=jax.ShapeDtypeStruct((lat_dev, members, length), jnp.float32),
        scratch_shapes=[
            pltpu.VMEM((wide, depth), jnp.float32),
            pltpu.VMEM((lat_dev, padded, 2 * depth), jnp.float32),
        ],
        compiler_params=pltpu.CompilerParams(dimension_semantics=("arbitrary",)),
        name="finish",
    )(summed, arrived, table)


def local(coeffs_old, noise, legendre, decay, amplitude, wavenumber_of_slot, lat_order):
    slots, parts, scales, members, width = coeffs_old.shape
    length = 2 * legendre.shape[1]
    gains = gains_of_slots(wavenumber_of_slot, decay, amplitude, slots)
    fresh = gains[:, None, :scales, None, :]
    keep = gains[:, None, scales : 2 * scales, None, :]
    coeffs_new = keep * coeffs_old + fresh * noise.astype(jnp.float32)
    turn = (0, 2, 3, 1, 4)
    summed, arrived, table = exchange(
        gains, coeffs_old.transpose(turn), noise.transpose(turn), legendre, wavenumber_of_slot, lat_order, length
    )
    pattern = finish(summed, arrived, table, slots, members)
    return (coeffs_new, pattern)


def solution(mesh):
    split_rows = ("lat", "lon")
    in_specs = (
        P(split_rows, None, None, None, None),
        P(split_rows, None, None, None, None),
        P(split_rows, None, None),
        P(),
        P(),
        P(),
        P(),
    )
    out_specs = (P(split_rows, None, None, None, None), P(split_rows, None, None))
    return jax.shard_map(local, mesh=mesh, in_specs=in_specs, out_specs=out_specs, check_vma=False)
```

time: 233 us -> 155 us (0.67)
  Pallas kernels: 54.9 us -> 139 us
  local copies, waits for them, and re-layouts: 80.4 us -> 1.28 us
  waiting for transfers between devices: 54.8 us -> 0 us
  matrix products: 14.2 us -> 0 us
  starting transfers between devices: 7.62 us -> 0 us
  other arithmetic: 17.3 us -> 13.7 us
    pallas_call x1 -> x3, Pallas kernels: 54.9 us -> 139 us  [the longest x1 126 us: exchange(): pl.pallas_call(functools.partial(exchange_kernel, first, middle, count, l...]
    all_to_all x1 -> x0, waiting for transfers between devices: 54.8 us -> none  [local(): lax.all_to_all(send, ('lat', 'lon'), split_axis=1, concat_axis=1, tiled=T...]
    unnamed x11 -> x0, local copies, waits for them, and re-layouts: 44 us -> none
    reshape x4 -> x0, local copies, waits for them, and re-layouts: 15.5 us -> none  [the longest x1 8.66 us: synthesis_table(): jnp.stack([weight * jnp.cos(angle), -weight * jnp.sin(angle)], axis=1)]
    dot_general x1 -> x0, matrix products: 14.2 us -> none  [local(): lax.dot_general(values, table, (((0,), (0,)), ((), ())), precision=lax.Pr...]
    mul x2 -> x0, other arithmetic: 14.1 us -> none  [the longest x1 14 us: synthesis_table(): weight * jnp.cos(angle)]
    add x0 -> x1, other arithmetic: none -> 13.7 us  [local(): coeffs_new = keep * coeffs_old + fresh * noise.astype(jnp.float32)]
    another operation x1 -> x0, local copies, waits for them, and re-layouts: 10.7 us -> none  [synthesis_table(): jnp.stack([weight * jnp.cos(angle), -weight * jnp.sin(angle)], axis=1)]
  transfers between devices with their start and end apart: 1 -> 0, of which waited for: 1 -> 0; matrix products, arithmetic and copies ran while one was open for 26% -> 0% of each run, Pallas kernels for 0% -> 0%
where the time goes in v2:
time: 155 us; the launch traced here: 154 us
  Pallas kernels  139 us (90%)
  other arithmetic  13.7 us (9%)
    pallas_call x1, Pallas kernels, exchange(): pl.pallas_call(functools.partial(exchange_kernel, first, middle, count, l...  126 us
    add x1, other arithmetic, local(): coeffs_new = keep * coeffs_old + fresh * noise.astype(jnp.float32)  13.7 us
    pallas_call x1, Pallas kernels, finish(): pl.pallas_call(functools.partial(finish_kernel, group, members), grid=(le...  9.16 us

profile of v2, /device:TPU:0, one launch (start us, length us, event | category | flops | bytes accessed | tf_op | source)
XLA Modules:
  0.0 154.3 jit_solution(16541278153420425868)
XLA Ops:
  0.6 3.1 %gains.1.gains_ref = f32[20,8,640]{2,1,0:T(8,128)} custom-call(s32[640]{0:T(1024)} %waves_ref.3, f32[3]{0:T(128)} %decay_ref.1, f32[3,640]{1,0:T(4,128)} %amplitude_ref.1), custom_call_target="tpu_custom_call" | custom-call | tf_op jit(solution)/shard_map/gains/pallas_call | solution.py:80
  3.7 1.3 fusion
  5.0 126.3 %exchange.1 = (f32[20,56,1280]{2,1,0:T(8,128)}, f32[32,8,512]{2,1,0:T(8,128)}, bf16[768,1280]{1,0:T(8,128)(2,1)}) custom-call(s32[640]{0:T(1024)} %order_ref.1, s32[640]{0:T(1024)} %waves_ref.3, f32[20,8,640]{2,1,0:T(8,128)} %gains.1.gains_ref, f32[20,3,50,2,640]{4,3,2,1,0:T(2,128)} %bitcast.2, bf16[20,3,50,2,640]{4,3,2,1,0:T(2,128)(2,1)} %bitcast.3, ...), custom_call_target="tpu_custom_call" | custom-call | tf_op jit(solution)/shard_map/exchange/pallas_call | solution.py:342
  131.3 9.2 %finish.1 = f32[20,50,1280]{2,1,0:T(8,128)} custom-call(f32[20,56,1280]{2,1,0:T(8,128)} %get-tuple-element.5.sum_ref, f32[32,8,512]{2,1,0:T(8,128)} %get-tuple-element.6.arrived_ref, bf16[768,1280]{1,0:T(8,128)(2,1)} %get-tuple-element.7.table_ref), custom_call_target="tpu_custom_call" | custom-call | tf_op jit(solution)/shard_map/finish/pallas_call | solution.py:398
  140.4 13.7 %multiply_add_fusion = f32[20,2,3,50,640]{4,1,3,2,0:T(2,128)} fusion(bf16[20,2,3,50,640]{4,1,3,2,0:T(2,128)(2,1)} %param.8, f32[20,2,3,50,640]{4,1,3,2,0:T(2,128)} %param.7, f32[20,3,640]{2,1,0:T(4,128)S(1)} %get-tuple-element.9, f32[20,3,640]{2,1,0:T(4,128)S(1)} %get-tuple-element.8), kind=kLoop, calls=%fused_computation | loop fusion | flops 15360000 | bytes 38707200 | tf_op jit(solution)/shard_map/add | solution.py:423

commit v3 on v2

--- a/solution.py
+++ b/solution.py
@@ -12,6 +12,8 @@
 SUBLANES = 8
 HALF = 64
 PARTS = 2
+VMEM_LIMIT = 40 << 20
+FINISH_LIMIT = 20 << 20
 MESH = pl.DeviceIdType.MESH
 
 
@@ -52,38 +54,6 @@
 def position():
     lat_size, lon_size = lax.axis_size("lat"), lax.axis_size("lon")
     return lax.axis_index("lat") * lon_size + lax.axis_index("lon"), lat_size * lon_size, lon_size
-
-
-def gains_kernel(waves_ref, decay_ref, amplitude_ref, gains_ref):
-    slots, _, width = gains_ref.shape
-    scales = amplitude_ref.shape[0]
-    me = position()[0]
-    row = lax.broadcasted_iota(jnp.int32, (SUBLANES, width), 0)
-    column = lax.broadcasted_iota(jnp.int32, (SUBLANES, width), 1)
-    table = jnp.zeros((SUBLANES, width), jnp.float32)
-    for scale in range(scales):
-        decay = jnp.full((1, width), decay_ref[scale], jnp.float32)
-        table = jnp.where(row == scale, amplitude_ref[scale : scale + 1, :] * jnp.sqrt(1.0 - decay * decay), table)
-        table = jnp.where(row == scales + scale, decay, table)
-
-    def one(slot, carry):
-        wave = waves_ref[me * slots + slot]
-        gains_ref[slot] = jnp.where(column + wave < width, pltpu.roll(table, width - wave, axis=1), 0.0)
-        return carry
-
-    lax.fori_loop(0, slots, one, 0)
-
-
-def gains_of_slots(waves, decay, amplitude, slots):
-    smem = pl.BlockSpec(memory_space=pltpu.SMEM)
-    vmem = pl.BlockSpec(memory_space=pltpu.VMEM)
-    return pl.pallas_call(
-        gains_kernel,
-        in_specs=[smem, smem, vmem],
-        out_specs=vmem,
-        out_shape=jax.ShapeDtypeStruct((slots, SUBLANES, amplitude.shape[1]), jnp.float32),
-        name="gains",
-    )(waves, decay, amplitude)
 
 
 def turn_block(block_ref, group, turned, left, lat_dev, members):
@@ -109,10 +79,10 @@
 
 def exchange_kernel(
     first, middle, count, last, members,
-    order_ref, waves_ref, gains_ref, old_hbm, noise_hbm, basis_hbm,
-    sum_hbm, arrived_hbm, table_hbm,
-    old, noise, basis, weights, field, send_first, send_middle, send_last, recv_first, recv_middle,
-    wave, turned, left, table, total, load_sem, own_sem, send_sem, recv_sem, out_sem,
+    order_ref, waves_ref, decay_ref, amplitude_ref, old_hbm, noise_hbm, basis_hbm,
+    new_hbm, sum_hbm, arrived_hbm, table_hbm,
+    old, noise, basis, new, base_gains, gains, weights, field, send_first, send_middle, send_last, recv_first, recv_middle,
+    wave, turned, left, table, total, load_sem, new_sem, own_sem, send_sem, recv_sem, out_sem,
 ):
     me, devices, lon_size = position()
     slots, lats, width = basis_hbm.shape
@@ -142,6 +112,17 @@
     for copy in loads(0):
         copy.start()
     weights[...] = jnp.zeros_like(weights)
+    base_gains[...] = jnp.zeros_like(base_gains)
+    for scale in range(scales):
+        decay = jnp.full((1, width), decay_ref[scale], jnp.float32)
+        base_gains[scale : scale + 1, :] = amplitude_ref[scale : scale + 1, :] * jnp.sqrt(1.0 - decay * decay)
+        base_gains[scales + scale : scales + scale + 1, :] = decay
+    column = lax.broadcasted_iota(jnp.int32, (SUBLANES, width), 1)
+
+    def store_new(slot):
+        side = lax.rem(slot, 2)
+        return pltpu.make_async_copy(new.at[side], new_hbm.at[slot], new_sem.at[side])
+
     if first.padded or middle.padded or last.padded:
         field[...] = jnp.zeros_like(field)
 
@@ -157,12 +138,21 @@
             for copy in loads(slot):
                 copy.wait()
             side = lax.rem(slot, 2)
+            wave_here = waves_ref[me * slots + slot]
+            gains[...] = jnp.where(column + wave_here < width, pltpu.roll(base_gains[...], width - wave_here, axis=1), 0.0)
+
+            @pl.when(slot > 1)
+            def _():
+                store_new(slot - 2).wait()
+
             summed = None
             for scale in range(scales):
-                fresh = gains_ref[slot, scale : scale + 1, :].reshape(1, 1, width)
-                keep = gains_ref[slot, scales + scale : scales + scale + 1, :].reshape(1, 1, width)
+                fresh = gains[scale : scale + 1, :].reshape(1, 1, width)
+                keep = gains[scales + scale : scales + scale + 1, :].reshape(1, 1, width)
                 value = keep * old[side, scale] + fresh * noise[side, scale].astype(jnp.float32)
+                new[side, scale] = value
                 summed = value if summed is None else summed + value
+            store_new(slot).start()
             for part in range(PARTS):
                 weights[part * HALF : part * HALF + members, :] = summed[:, part, :]
             high, low = split(weights[...])
@@ -243,6 +233,8 @@
     lax.fori_loop(0, count, middle_step, 0)
     transform(last, slots - last.size)
     pack_and_send(last, send_last, arrived_hbm, final)
+    for slot in range(max(slots - 2, 0), slots):
+        store_new(slot).wait()
 
     def make_table(group, start):
         rows = group.rows
@@ -326,7 +318,7 @@
     await_group(arrived_hbm, final)
 
 
-def exchange(gains, old, noise, legendre, waves, lat_order, length):
+def exchange(old, noise, legendre, decay, amplitude, waves, lat_order, length):
     devices = lax.axis_size("lat") * lax.axis_size("lon")
     slots, scales, members, parts, width = old.shape
     lats = legendre.shape[1]
@@ -339,11 +331,13 @@
     some = max(count, 1)
     smem = pl.BlockSpec(memory_space=pltpu.SMEM)
     anywhere = pl.BlockSpec(memory_space=pl.ANY)
+    hbm = pl.BlockSpec(memory_space=pltpu.HBM)
     return pl.pallas_call(
         functools.partial(exchange_kernel, first, middle, count, last, members),
-        in_specs=[smem, smem, pl.BlockSpec(memory_space=pltpu.VMEM), anywhere, anywhere, anywhere],
-        out_specs=[anywhere, anywhere, anywhere],
+        in_specs=[smem, smem, smem, pl.BlockSpec(memory_space=pltpu.VMEM), hbm, hbm, hbm],
+        out_specs=[anywhere, anywhere, anywhere, anywhere],
         out_shape=[
+            jax.ShapeDtypeStruct(old.shape, jnp.float32),
             jax.ShapeDtypeStruct((lat_dev, padded, length), jnp.float32),
             jax.ShapeDtypeStruct(last.block(devices), jnp.float32),
             jax.ShapeDtypeStruct((3 * devices * last.rows, length), jnp.bfloat16),
@@ -352,6 +346,9 @@
             pltpu.VMEM((2, scales, members, parts, width), jnp.float32),
             pltpu.VMEM((2, scales, members, parts, width), jnp.bfloat16),
             pltpu.VMEM((2, lats, width), jnp.float32),
+            pltpu.VMEM((2, scales, members, parts, width), jnp.float32),
+            pltpu.VMEM((SUBLANES, width), jnp.float32),
+            pltpu.VMEM((SUBLANES, width), jnp.float32),
             pltpu.VMEM((LANES, width), jnp.float32),
             pltpu.VMEM((lats, rows, LANES), jnp.float32),
             pltpu.VMEM(first.block(devices), jnp.float32),
@@ -365,27 +362,31 @@
             pltpu.VMEM((3 * depth, length), jnp.bfloat16),
             pltpu.VMEM((lat_dev, padded, length), jnp.float32),
             pltpu.SemaphoreType.DMA((3, 2)),
+            pltpu.SemaphoreType.DMA((2,)),
             pltpu.SemaphoreType.DMA((count + 2,)),
             pltpu.SemaphoreType.DMA((count + 2,)),
             pltpu.SemaphoreType.DMA((count + 2,)),
             pltpu.SemaphoreType.DMA((2,)),
         ],
-        compiler_params=pltpu.CompilerParams(collective_id=0, has_side_effects=True),
+        compiler_params=pltpu.CompilerParams(collective_id=0, has_side_effects=True, vmem_limit_bytes=VMEM_LIMIT),
         name="exchange",
-    )(lat_order, waves, gains, old, noise, legendre)
+    )(lat_order, waves, decay, amplitude, old, noise, legendre)
 
 
 def finish_kernel(group, members, sum_ref, arrived_ref, table_ref, out_ref, turned, left):
-    lat_dev, padded, chunk = sum_ref.shape
+    lat_dev, padded, _ = sum_ref.shape
+    chunk = out_ref.shape[2]
     depth = left.shape[2] // 2
-
-    @pl.when(pl.program_id(0) == 0)
+    step = pl.program_id(0)
+
+    @pl.when(step == 0)
     def _():
         left[...] = jnp.zeros_like(left)
         turn_block(arrived_ref, group, turned, left, lat_dev, members)
 
+    span = pl.ds(pl.multiple_of(step * chunk, chunk), chunk)
     values = left[...].reshape(lat_dev * padded, 2 * depth).astype(jnp.bfloat16)
-    part = sum_ref[...] + contract(values, table_ref[...], depth).reshape(lat_dev, padded, chunk)
+    part = sum_ref[:, :, span] + contract(values, table_ref[:, span], depth).reshape(lat_dev, padded, chunk)
     out_ref[...] = part[:, :members, :]
 
 
@@ -395,21 +396,18 @@
     devices, rows, wide = arrived.shape
     depth = devices * rows
     chunk = 2 * LANES
+    vmem = pl.BlockSpec(memory_space=pltpu.VMEM)
     return pl.pallas_call(
         functools.partial(finish_kernel, group, members),
         grid=(length // chunk,),
-        in_specs=[
-            pl.BlockSpec((lat_dev, padded, chunk), lambda n: (0, 0, n)),
-            pl.BlockSpec((devices, rows, wide), lambda n: (0, 0, 0)),
-            pl.BlockSpec((3 * depth, chunk), lambda n: (0, n)),
-        ],
+        in_specs=[vmem, vmem, vmem],
         out_specs=pl.BlockSpec((lat_dev, members, chunk), lambda n: (0, 0, n)),
         out_shape=jax.ShapeDtypeStruct((lat_dev, members, length), jnp.float32),
         scratch_shapes=[
             pltpu.VMEM((wide, depth), jnp.float32),
             pltpu.VMEM((lat_dev, padded, 2 * depth), jnp.float32),
         ],
-        compiler_params=pltpu.CompilerParams(dimension_semantics=("arbitrary",)),
+        compiler_params=pltpu.CompilerParams(dimension_semantics=("arbitrary",), vmem_limit_bytes=FINISH_LIMIT),
         name="finish",
     )(summed, arrived, table)
 
@@ -417,14 +415,11 @@
 def local(coeffs_old, noise, legendre, decay, amplitude, wavenumber_of_slot, lat_order):
     slots, parts, scales, members, width = coeffs_old.shape
     length = 2 * legendre.shape[1]
-    gains = gains_of_slots(wavenumber_of_slot, decay, amplitude, slots)
-    fresh = gains[:, None, :scales, None, :]
-    keep = gains[:, None, scales : 2 * scales, None, :]
-    coeffs_new = keep * coeffs_old + fresh * noise.astype(jnp.float32)
     turn = (0, 2, 3, 1, 4)
-    summed, arrived, table = exchange(
-        gains, coeffs_old.transpose(turn), noise.transpose(turn), legendre, wavenumber_of_slot, lat_order, length
+    new, summed, arrived, table = exchange(
+        coeffs_old.transpose(turn), noise.transpose(turn), legendre, decay, amplitude, wavenumber_of_slot, lat_order, length
     )
+    coeffs_new = new.transpose(0, 3, 1, 2, 4)
     pattern = finish(summed, arrived, table, slots, members)
     return (coeffs_new, pattern)
 

time: 155 us -> 147 us (0.948)
  other arithmetic: 13.7 us -> 0 us
  local copies, waits for them, and re-layouts: 1.28 us -> 14.1 us
  Pallas kernels: 139 us -> 132 us
    unnamed x0 -> x9, local copies, waits for them, and re-layouts: none -> 14.1 us
    add x1 -> x0, other arithmetic: 13.7 us -> none  [local(): coeffs_new = keep * coeffs_old + fresh * noise.astype(jnp.float32)]
    pallas_call x1, Pallas kernels: 9.16 us -> 5.35 us  [finish(): pl.pallas_call(functools.partial(finish_kernel, group, members), grid=(le...]
    pallas_call x1 -> x0, Pallas kernels: 3.06 us -> none  [gains_of_slots(): pl.pallas_call(gains_kernel, in_specs=[smem, smem, vmem], out_specs=vmem,...]
where the time goes in v3:
time: 147 us; the launch traced here: 146 us
  Pallas kernels  132 us (90%)
  local copies, waits for them, and re-layouts  14.1 us (10%)
    pallas_call x1, Pallas kernels, exchange(): pl.pallas_call(functools.partial(exchange_kernel, first, middle, count, l...  126 us
    unnamed x9, local copies, waits for them, and re-layouts  14.1 us
    pallas_call x1, Pallas kernels, finish(): pl.pallas_call(functools.partial(finish_kernel, group, members), grid=(le...  5.35 us

profile of v3, /device:TPU:0, one launch (start us, length us, event | category | flops | bytes accessed | tf_op | source)
XLA Modules:
  0.0 146.3 jit_solution(524489050100679003)
XLA Ops:
  0.6 0.0 copy-start
  0.6 0.7 copy-done
  1.3 0.0 copy-start.1
  1.3 0.7 copy-done.1
  2.0 0.0 copy-start.2
  2.0 0.7 copy-done.2
  2.7 0.0 copy-start.3
  2.7 0.7 copy-done.3
  3.4 126.2 %exchange.1 = (f32[20,3,50,2,640]{4,3,2,1,0:T(2,128)}, f32[20,56,1280]{2,1,0:T(8,128)S(1)}, f32[32,8,512]{2,1,0:T(8,128)S(1)}, bf16[768,1280]{1,0:T(8,128)(2,1)S(1)}) custom-call(s32[640]{0:T(1024)S(1)} %copy-done.1, s32[640]{0:T(1024)S(1)} %copy-done.2, f32[3]{0:T(128)S(1)} %copy-done.3, f32[3,640]{1,0:T(4,128)S(1)} %copy-done, ...), custom_call_target="tpu_custom_call" | custom-call | tf_op jit(solution)/shard_map/exchange/pallas_call | solution.py:335
  129.6 5.4 %finish.1 = f32[20,50,1280]{2,1,0:T(8,128)} custom-call(f32[20,56,1280]{2,1,0:T(8,128)S(1)} %get-tuple-element.7.sum_ref, f32[32,8,512]{2,1,0:T(8,128)S(1)} %get-tuple-element.8.arrived_ref, bf16[768,1280]{1,0:T(8,128)(2,1)S(1)} %get-tuple-element.9.table_ref), custom_call_target="tpu_custom_call" | custom-call | tf_op jit(solution)/shard_map/finish/pallas_call | solution.py:400
  135.0 11.4 %copy.10 = f32[20,2,3,50,640]{4,1,3,2,0:T(2,128)} copy(f32[20,2,3,50,640]{4,1,3,2,0:T(2,128)} %bitcast.4) | data formatting | bytes 30720000
Async XLA Ops:
  0.6 0.7 copy-start
  1.3 0.7 copy-start.1
  2.0 0.7 copy-start.2
  2.7 0.7 copy-start.3

commit v4 on v3

--- a/solution.py
+++ b/solution.py
@@ -12,8 +12,8 @@
 SUBLANES = 8
 HALF = 64
 PARTS = 2
-VMEM_LIMIT = 40 << 20
-FINISH_LIMIT = 20 << 20
+VMEM_LIMIT = 28 << 20
+FINISH_LIMIT = 16 << 20
 MESH = pl.DeviceIdType.MESH
 
 
@@ -42,13 +42,13 @@
 
 def plan(slots, lat_dev, members):
     if slots % 4 == 0 and slots >= 8:
-        sizes = (2, 4, slots // 4 - 1, 2)
-    elif slots > 4 and slots % 4:
-        sizes = (slots % 4, 4, slots // 4 - 1, 4)
+        sizes, size = (1, 1, 2), 4
+    elif slots > 4:
+        sizes, size = (slots % 4,), 4
     else:
-        sizes = (1, 1, slots - 2, 1)
-    first, middle, count, last = sizes
-    return Group(first, lat_dev, members), Group(middle, lat_dev, members), count, Group(last, lat_dev, members)
+        sizes, size = (), 1
+    leaders = [Group(size_, lat_dev, members) for size_ in sizes]
+    return leaders, Group(size, lat_dev, members), (slots - sum(sizes)) // size
 
 
 def position():
@@ -78,17 +78,22 @@
 
 
 def exchange_kernel(
-    first, middle, count, last, members,
+    leaders, middle, count, members,
     order_ref, waves_ref, decay_ref, amplitude_ref, old_hbm, noise_hbm, basis_hbm,
-    new_hbm, sum_hbm, arrived_hbm, table_hbm,
-    old, noise, basis, new, base_gains, gains, weights, field, send_first, send_middle, send_last, recv_first, recv_middle,
-    wave, turned, left, table, total, load_sem, new_sem, own_sem, send_sem, recv_sem, out_sem,
+    *refs,
 ):
+    scales = old_hbm.shape[1]
+    new = refs[:scales]
+    (
+        total, recv_middle, table,
+        old, noise, basis, base_gains, gains, weights, field, send_lead, recv_lead, send_middle,
+        wave, turned, left, load_sem, own_sem, send_sem, recv_sem,
+    ) = refs[scales:]
     me, devices, lon_size = position()
     slots, lats, width = basis_hbm.shape
-    scales = old_hbm.shape[1]
     lat_dev, padded, length = total.shape
-    final = count + 1
+    lead = len(leaders)
+    starts = [sum(group.size for group in leaders[:index]) for index in range(lead + 1)]
 
     def peer(other):
         return other // lon_size, lax.rem(other, lon_size)
@@ -119,11 +124,7 @@
         base_gains[scales + scale : scales + scale + 1, :] = decay
     column = lax.broadcasted_iota(jnp.int32, (SUBLANES, width), 1)
 
-    def store_new(slot):
-        side = lax.rem(slot, 2)
-        return pltpu.make_async_copy(new.at[side], new_hbm.at[slot], new_sem.at[side])
-
-    if first.padded or middle.padded or last.padded:
+    if any(group.padded for group in leaders + [middle]):
         field[...] = jnp.zeros_like(field)
 
     def transform(group, start):
@@ -141,18 +142,13 @@
             wave_here = waves_ref[me * slots + slot]
             gains[...] = jnp.where(column + wave_here < width, pltpu.roll(base_gains[...], width - wave_here, axis=1), 0.0)
 
-            @pl.when(slot > 1)
-            def _():
-                store_new(slot - 2).wait()
-
             summed = None
             for scale in range(scales):
                 fresh = gains[scale : scale + 1, :].reshape(1, 1, width)
                 keep = gains[scales + scale : scales + scale + 1, :].reshape(1, 1, width)
                 value = keep * old[side, scale] + fresh * noise[side, scale].astype(jnp.float32)
-                new[side, scale] = value
+                new[scale][slot] = value
                 summed = value if summed is None else summed + value
-            store_new(slot).start()
             for part in range(PARTS):
                 weights[part * HALF : part * HALF + members, :] = summed[:, part, :]
             high, low = split(weights[...])
@@ -221,20 +217,20 @@
         pltpu.make_async_copy(others, others, recv_sem.at[index]).wait()
         pltpu.make_async_copy(recv.at[0], recv.at[0], own_sem.at[index]).wait()
 
-    transform(first, 0)
-    pl.semaphore_wait(barrier, devices - 1)
-    pack_and_send(first, send_first, recv_first, 0)
+    for index, group in enumerate(leaders):
+        transform(group, starts[index])
+        if index == 0:
+            pl.semaphore_wait(barrier, devices - 1)
+        pack_and_send(group, send_lead[index], recv_lead[index], index)
+    if not leaders:
+        pl.semaphore_wait(barrier, devices - 1)
 
     def middle_step(step, carry):
-        transform(middle, first.size + step * middle.size)
-        pack_and_send(middle, send_middle.at[step], recv_middle.at[step], step + 1)
+        transform(middle, starts[lead] + step * middle.size)
+        pack_and_send(middle, send_middle.at[step], recv_middle.at[step], step + lead)
         return carry
 
     lax.fori_loop(0, count, middle_step, 0)
-    transform(last, slots - last.size)
-    pack_and_send(last, send_last, arrived_hbm, final)
-    for slot in range(max(slots - 2, 0), slots):
-        store_new(slot).wait()
 
     def make_table(group, start):
         rows = group.rows
@@ -271,9 +267,8 @@
             table[depth : 2 * depth, span] = high
             table[2 * depth : 3 * depth, span] = low
 
-    def synthesis(group, recv, index, start, fresh):
+    def synthesis(group, recv, index):
         depth = devices * group.rows
-        make_table(group, start)
         await_group(recv, index)
         turn_block(recv, group, turned, left, lat_dev, members)
         values = left[:, :, : 2 * depth].reshape(lat_dev * padded, 2 * depth).astype(jnp.bfloat16)
@@ -281,41 +276,41 @@
 
         def columns(n, carry):
             span = pl.ds(pl.multiple_of(n * chunk, chunk), chunk)
-            part = contract(values, table[: 3 * depth, span], depth).reshape(lat_dev, padded, chunk)
-            total[:, :, span] = part if fresh else total[:, :, span] + part
+            total[:, :, span] += contract(values, table[: 3 * depth, span], depth).reshape(lat_dev, padded, chunk)
             return carry
 
         lax.fori_loop(0, length // chunk, columns, 0)
 
     left[...] = jnp.zeros_like(left)
-    synthesis(first, recv_first, 0, 0, True)
+    total[...] = jnp.zeros_like(total)
+    for index, group in enumerate(leaders):
+        make_table(group, starts[index])
+        synthesis(group, recv_lead[index], index)
 
     def middle_synthesis(step, carry):
-        synthesis(middle, recv_middle.at[step], step + 1, first.size + step * middle.size, False)
+        make_table(middle, starts[lead] + step * middle.size)
+
+        @pl.when(step < count - 1)
+        def _():
+            synthesis(middle, recv_middle.at[step], step + lead)
+
         return carry
 
     lax.fori_loop(0, count, middle_synthesis, 0)
-    sum_out = pltpu.make_async_copy(total, sum_hbm, out_sem.at[0])
-    sum_out.start()
-    make_table(last, slots - last.size)
-    table_out = pltpu.make_async_copy(table.at[: table_hbm.shape[0]], table_hbm, out_sem.at[1])
-    table_out.start()
 
     def sent(block, index):
         others = block.at[pl.ds(0, devices - 1)]
         pltpu.make_async_copy(others, others, send_sem.at[index]).wait()
 
-    sent(send_first, 0)
+    for index in range(lead):
+        sent(send_lead[index], index)
 
     def middle_sent(step, carry):
-        sent(send_middle.at[step], step + 1)
+        sent(send_middle.at[step], step + lead)
         return carry
 
     lax.fori_loop(0, count, middle_sent, 0)
-    sum_out.wait()
-    table_out.wait()
-    sent(send_last, final)
-    await_group(arrived_hbm, final)
+    await_group(recv_middle.at[count - 1], lead + count - 1)
 
 
 def exchange(old, noise, legendre, decay, amplitude, waves, lat_order, length):
@@ -323,104 +318,116 @@
     slots, scales, members, parts, width = old.shape
     lats = legendre.shape[1]
     lat_dev = lats // devices
-    first, middle, count, last = plan(slots, lat_dev, members)
-    groups = (first, middle, last)
+    leaders, middle, count = plan(slots, lat_dev, members)
+    groups = leaders + [middle]
+    lead_blocks = tuple(pltpu.VMEM(group.block(devices), jnp.float32) for group in leaders)
     padded = round_up(members, SUBLANES)
-    depth = devices * max(group.rows for group in groups)
     rows = max(group.rows for group in groups)
-    some = max(count, 1)
+    depth = devices * rows
     smem = pl.BlockSpec(memory_space=pltpu.SMEM)
-    anywhere = pl.BlockSpec(memory_space=pl.ANY)
+    vmem = pl.BlockSpec(memory_space=pltpu.VMEM)
     hbm = pl.BlockSpec(memory_space=pltpu.HBM)
+    large = [pltpu.with_memory_space_constraint(array, pltpu.HBM) for array in (old, noise, legendre)]
     return pl.pallas_call(
-        functools.partial(exchange_kernel, first, middle, count, last, members),
-        in_specs=[smem, smem, smem, pl.BlockSpec(memory_space=pltpu.VMEM), hbm, hbm, hbm],
-        out_specs=[anywhere, anywhere, anywhere, anywhere],
-        out_shape=[
-            jax.ShapeDtypeStruct(old.shape, jnp.float32),
-            jax.ShapeDtypeStruct((lat_dev, padded, length), jnp.float32),
-            jax.ShapeDtypeStruct(last.block(devices), jnp.float32),
-            jax.ShapeDtypeStruct((3 * devices * last.rows, length), jnp.bfloat16),
+        functools.partial(exchange_kernel, leaders, middle, count, members),
+        in_specs=[smem, smem, smem, vmem, hbm, hbm, hbm],
+        out_specs=[vmem] * (scales + 3),
+        out_shape=[pltpu.VMEM((slots, members, parts, width), jnp.float32)] * scales
+        + [
+            pltpu.VMEM((lat_dev, padded, length), jnp.float32),
+            pltpu.VMEM((count,) + middle.block(devices), jnp.float32),
+            pltpu.VMEM((3 * depth, length), jnp.bfloat16),
         ],
         scratch_shapes=[
             pltpu.VMEM((2, scales, members, parts, width), jnp.float32),
             pltpu.VMEM((2, scales, members, parts, width), jnp.bfloat16),
             pltpu.VMEM((2, lats, width), jnp.float32),
-            pltpu.VMEM((2, scales, members, parts, width), jnp.float32),
             pltpu.VMEM((SUBLANES, width), jnp.float32),
             pltpu.VMEM((SUBLANES, width), jnp.float32),
             pltpu.VMEM((LANES, width), jnp.float32),
             pltpu.VMEM((lats, rows, LANES), jnp.float32),
-            pltpu.VMEM(first.block(devices), jnp.float32),
-            pltpu.VMEM((some,) + middle.block(devices), jnp.float32),
-            pltpu.VMEM(last.block(devices), jnp.float32),
-            pltpu.VMEM(first.block(devices), jnp.float32),
-            pltpu.VMEM((some,) + middle.block(devices), jnp.float32),
+            lead_blocks,
+            lead_blocks,
+            pltpu.VMEM((count,) + middle.block(devices), jnp.float32),
             pltpu.VMEM((depth, LANES), jnp.float32),
             pltpu.VMEM((max(group.wide for group in groups), depth), jnp.float32),
             pltpu.VMEM((lat_dev, padded, 2 * depth), jnp.float32),
-            pltpu.VMEM((3 * depth, length), jnp.bfloat16),
-            pltpu.VMEM((lat_dev, padded, length), jnp.float32),
             pltpu.SemaphoreType.DMA((3, 2)),
-            pltpu.SemaphoreType.DMA((2,)),
-            pltpu.SemaphoreType.DMA((count + 2,)),
-            pltpu.SemaphoreType.DMA((count + 2,)),
-            pltpu.SemaphoreType.DMA((count + 2,)),
-            pltpu.SemaphoreType.DMA((2,)),
+            pltpu.SemaphoreType.DMA((len(leaders) + count,)),
+            pltpu.SemaphoreType.DMA((len(leaders) + count,)),
+            pltpu.SemaphoreType.DMA((len(leaders) + count,)),
         ],
         compiler_params=pltpu.CompilerParams(collective_id=0, has_side_effects=True, vmem_limit_bytes=VMEM_LIMIT),
         name="exchange",
-    )(lat_order, waves, decay, amplitude, old, noise, legendre)
-
-
-def finish_kernel(group, members, sum_ref, arrived_ref, table_ref, out_ref, turned, left):
+    )(lat_order, waves, decay, amplitude, *large)
+
+
+def finish_kernel(group, members, scales, *refs):
+    new = refs[:scales]
+    sum_ref, arrived_ref, table_ref, out_ref, new_out, turned, left, copy_sem = refs[scales:]
     lat_dev, padded, _ = sum_ref.shape
     chunk = out_ref.shape[2]
     depth = left.shape[2] // 2
     step = pl.program_id(0)
 
+    def writes():
+        return [pltpu.make_async_copy(ref, new_out.at[:, scale], copy_sem.at[scale]) for scale, ref in enumerate(new)]
+
     @pl.when(step == 0)
     def _():
+        for copy in writes():
+            copy.start()
         left[...] = jnp.zeros_like(left)
-        turn_block(arrived_ref, group, turned, left, lat_dev, members)
+        turn_block(arrived_ref.at[arrived_ref.shape[0] - 1], group, turned, left, lat_dev, members)
 
     span = pl.ds(pl.multiple_of(step * chunk, chunk), chunk)
     values = left[...].reshape(lat_dev * padded, 2 * depth).astype(jnp.bfloat16)
-    part = sum_ref[:, :, span] + contract(values, table_ref[:, span], depth).reshape(lat_dev, padded, chunk)
+    part = sum_ref[:, :, span] + contract(values, table_ref[: 3 * depth, span], depth).reshape(lat_dev, padded, chunk)
     out_ref[...] = part[:, :members, :]
 
-
-def finish(summed, arrived, table, slots, members):
+    @pl.when(step == pl.num_programs(0) - 1)
+    def _():
+        for copy in writes():
+            copy.wait()
+
+
+def finish(new, summed, arrived, table):
     lat_dev, padded, length = summed.shape
-    group = plan(slots, lat_dev, members)[3]
-    devices, rows, wide = arrived.shape
+    scales = len(new)
+    slots, members, parts, width = new[0].shape
+    group = plan(slots, lat_dev, members)[1]
+    _, devices, rows, wide = arrived.shape
     depth = devices * rows
     chunk = 2 * LANES
     vmem = pl.BlockSpec(memory_space=pltpu.VMEM)
     return pl.pallas_call(
-        functools.partial(finish_kernel, group, members),
+        functools.partial(finish_kernel, group, members, scales),
         grid=(length // chunk,),
-        in_specs=[vmem, vmem, vmem],
-        out_specs=pl.BlockSpec((lat_dev, members, chunk), lambda n: (0, 0, n)),
-        out_shape=jax.ShapeDtypeStruct((lat_dev, members, length), jnp.float32),
+        in_specs=[vmem] * (scales + 3),
+        out_specs=[pl.BlockSpec((lat_dev, members, chunk), lambda n: (0, 0, n)), pl.BlockSpec(memory_space=pl.ANY)],
+        out_shape=[
+            jax.ShapeDtypeStruct((lat_dev, members, length), jnp.float32),
+            jax.ShapeDtypeStruct((slots, scales, members, parts, width), jnp.float32),
+        ],
         scratch_shapes=[
             pltpu.VMEM((wide, depth), jnp.float32),
             pltpu.VMEM((lat_dev, padded, 2 * depth), jnp.float32),
+            pltpu.SemaphoreType.DMA((scales,)),
         ],
         compiler_params=pltpu.CompilerParams(dimension_semantics=("arbitrary",), vmem_limit_bytes=FINISH_LIMIT),
         name="finish",
-    )(summed, arrived, table)
+    )(*[pltpu.with_memory_space_constraint(array, pltpu.VMEM) for array in (*new, summed, arrived, table)])
 
 
 def local(coeffs_old, noise, legendre, decay, amplitude, wavenumber_of_slot, lat_order):
     slots, parts, scales, members, width = coeffs_old.shape
     length = 2 * legendre.shape[1]
     turn = (0, 2, 3, 1, 4)
-    new, summed, arrived, table = exchange(
+    *new, summed, arrived, table = exchange(
         coeffs_old.transpose(turn), noise.transpose(turn), legendre, decay, amplitude, wavenumber_of_slot, lat_order, length
     )
+    pattern, new = finish(new, summed, arrived, table)
     coeffs_new = new.transpose(0, 3, 1, 2, 4)
-    pattern = finish(summed, arrived, table, slots, members)
     return (coeffs_new, pattern)
 
 

time: 147 us -> 137 us (0.932)
  local copies, waits for them, and re-layouts: 14.1 us -> 0 us
  Pallas kernels: 132 us -> 136 us
    unnamed x9 -> x0, local copies, waits for them, and re-layouts: 14.1 us -> none
    pallas_call x2, Pallas kernels: 132 us -> 136 us  [the longest x1 127 us: exchange(): pl.pallas_call(functools.partial(exchange_kernel, leaders, middle, count,...]
where the time goes in v4:
time: 137 us
  Pallas kernels  136 us (99%)
    pallas_call x1, Pallas kernels, exchange(): pl.pallas_call(functools.partial(exchange_kernel, leaders, middle, count,...  127 us
    pallas_call x1, Pallas kernels, finish(): pl.pallas_call(functools.partial(finish_kernel, group, members, scales),...  9.14 us

profile of v4, /device:TPU:0, one launch (start us, length us, event | category | flops | bytes accessed | tf_op | source)
XLA Modules:
  0.0 136.9 jit_solution(2272814435910554222)
XLA Ops:
  0.6 126.9 %exchange.1 = (f32[20,50,2,640]{3,2,1,0:T(2,128)S(1)}, f32[20,50,2,640]{3,2,1,0:T(2,128)S(1)}, f32[20,50,2,640]{3,2,1,0:T(2,128)S(1)}, f32[20,56,1280]{2,1,0:T(8...) custom-call(s32[640]{0:T(1024)} %order_ref.1, s32[640]{0:T(1024)} %waves_ref.1, f32[3]{0:T(128)} %decay_ref.1, ...), custom_call_target="tpu_custom_call" | custom-call | tf_op jit(solution)/shard_map/exchange/pallas_call | solution.py:331
  127.5 9.1 %finish.1 = (f32[20,50,1280]{2,1,0:T(8,128)}, f32[20,3,50,2,640]{4,3,2,1,0:T(2,128)}) custom-call(f32[20,50,2,640]{3,2,1,0:T(2,128)S(1)} %get-tuple-element.10.refs_0_, f32[20,50,2,640]{3,2,1,0:T(2,128)S(1)} %get-tuple-element.11.refs_1_, f32[20,50,2,640]{3,2,1,0:T(2,128)S(1)} %get-tuple-element.12.refs_2_, f32[20,56,1280]{2,1,0:T(8,128)S(1)} %get-tuple-element.13.refs_3_, ...), custom_call_target="tpu_custom_call" | custom-call | tf_op jit(solution)/shard_map/finish/pallas_call | solution.py:403

commit v5 on v4

--- a/solution.py
+++ b/solution.py
@@ -79,13 +79,14 @@
 
 def exchange_kernel(
     leaders, middle, count, members,
-    order_ref, waves_ref, decay_ref, amplitude_ref, old_hbm, noise_hbm, basis_hbm,
+    order_hbm, waves_hbm, decay_hbm, amplitude_hbm, old_hbm, noise_hbm, basis_hbm,
     *refs,
 ):
     scales = old_hbm.shape[1]
     new = refs[:scales]
     (
         total, recv_middle, table,
+        order_ref, waves_ref, decay_ref, amplitude_ref, small_sem,
         old, noise, basis, base_gains, gains, weights, field, send_lead, recv_lead, send_middle,
         wave, turned, left, load_sem, own_sem, send_sem, recv_sem,
     ) = refs[scales:]
@@ -98,14 +99,6 @@
     def peer(other):
         return other // lon_size, lax.rem(other, lon_size)
 
-    barrier = pltpu.get_barrier_semaphore()
-
-    def greet(k, carry):
-        pl.semaphore_signal(barrier, inc=1, device_id=peer(lax.rem(me + k, devices)), device_id_type=MESH)
-        return carry
-
-    lax.fori_loop(1, devices, greet, 0)
-
     def loads(slot):
         side = lax.rem(slot, 2)
         return (
@@ -114,10 +107,27 @@
             pltpu.make_async_copy(basis_hbm.at[slot], basis.at[side], load_sem.at[2, side]),
         )
 
+    small = [
+        pltpu.make_async_copy(source, target, small_sem.at[index])
+        for index, (source, target) in enumerate(
+            ((decay_hbm, decay_ref), (amplitude_hbm, amplitude_ref), (waves_hbm, waves_ref), (order_hbm, order_ref))
+        )
+    ]
+    for copy in small:
+        copy.start()
     for copy in loads(0):
         copy.start()
+    barrier = pltpu.get_barrier_semaphore()
+
+    def greet(k, carry):
+        pl.semaphore_signal(barrier, inc=1, device_id=peer(lax.rem(me + k, devices)), device_id_type=MESH)
+        return carry
+
+    lax.fori_loop(1, devices, greet, 0)
     weights[...] = jnp.zeros_like(weights)
     base_gains[...] = jnp.zeros_like(base_gains)
+    for copy in small:
+        copy.wait()
     for scale in range(scales):
         decay = jnp.full((1, width), decay_ref[scale], jnp.float32)
         base_gains[scale : scale + 1, :] = amplitude_ref[scale : scale + 1, :] * jnp.sqrt(1.0 - decay * decay)
@@ -136,8 +146,9 @@
                 for copy in loads(slot + 1):
                     copy.start()
 
-            for copy in loads(slot):
-                copy.wait()
+            old_load, noise_load, basis_load = loads(slot)
+            old_load.wait()
+            noise_load.wait()
             side = lax.rem(slot, 2)
             wave_here = waves_ref[me * slots + slot]
             gains[...] = jnp.where(column + wave_here < width, pltpu.roll(base_gains[...], width - wave_here, axis=1), 0.0)
@@ -152,6 +163,7 @@
             for part in range(PARTS):
                 weights[part * HALF : part * HALF + members, :] = summed[:, part, :]
             high, low = split(weights[...])
+            basis_load.wait()
             basis_high, basis_low = split(basis[side])
             lanes = (((1,), (1,)), ((), ()))
             pair = lax.dot_general(basis_high, jnp.concatenate([high, low], axis=0), lanes, preferred_element_type=jnp.float32)
@@ -324,13 +336,13 @@
     padded = round_up(members, SUBLANES)
     rows = max(group.rows for group in groups)
     depth = devices * rows
-    smem = pl.BlockSpec(memory_space=pltpu.SMEM)
     vmem = pl.BlockSpec(memory_space=pltpu.VMEM)
     hbm = pl.BlockSpec(memory_space=pltpu.HBM)
-    large = [pltpu.with_memory_space_constraint(array, pltpu.HBM) for array in (old, noise, legendre)]
+    operands = (lat_order, waves, decay, amplitude, old, noise, legendre)
+    operands = [pltpu.with_memory_space_constraint(array, pltpu.HBM) for array in operands]
     return pl.pallas_call(
         functools.partial(exchange_kernel, leaders, middle, count, members),
-        in_specs=[smem, smem, smem, vmem, hbm, hbm, hbm],
+        in_specs=[hbm] * len(operands),
         out_specs=[vmem] * (scales + 3),
         out_shape=[pltpu.VMEM((slots, members, parts, width), jnp.float32)] * scales
         + [
@@ -339,6 +351,11 @@
             pltpu.VMEM((3 * depth, length), jnp.bfloat16),
         ],
         scratch_shapes=[
+            pltpu.SMEM(lat_order.shape, jnp.int32),
+            pltpu.SMEM(waves.shape, jnp.int32),
+            pltpu.SMEM(decay.shape, jnp.float32),
+            pltpu.VMEM(amplitude.shape, jnp.float32),
+            pltpu.SemaphoreType.DMA((4,)),
             pltpu.VMEM((2, scales, members, parts, width), jnp.float32),
             pltpu.VMEM((2, scales, members, parts, width), jnp.bfloat16),
             pltpu.VMEM((2, lats, width), jnp.float32),
@@ -359,24 +376,29 @@
         ],
         compiler_params=pltpu.CompilerParams(collective_id=0, has_side_effects=True, vmem_limit_bytes=VMEM_LIMIT),
         name="exchange",
-    )(lat_order, waves, decay, amplitude, *large)
+    )(*operands)
 
 
 def finish_kernel(group, members, scales, *refs):
     new = refs[:scales]
     sum_ref, arrived_ref, table_ref, out_ref, new_out, turned, left, copy_sem = refs[scales:]
-    lat_dev, padded, _ = sum_ref.shape
+    lat_dev, padded, length = sum_ref.shape
     chunk = out_ref.shape[2]
     depth = left.shape[2] // 2
     step = pl.program_id(0)
 
-    def writes():
-        return [pltpu.make_async_copy(ref, new_out.at[:, scale], copy_sem.at[scale]) for scale, ref in enumerate(new)]
+    slots = new_out.shape[0]
+    share = -(-slots // (length // chunk - 1))
+
+    def write(slot, carry):
+        for scale, ref in enumerate(new):
+            pltpu.make_async_copy(ref.at[slot], new_out.at[slot, scale], copy_sem.at[scale]).start()
+        return carry
+
+    lax.fori_loop(jnp.minimum(share * step, slots), jnp.minimum(share * (step + 1), slots), write, 0)
 
     @pl.when(step == 0)
     def _():
-        for copy in writes():
-            copy.start()
         left[...] = jnp.zeros_like(left)
         turn_block(arrived_ref.at[arrived_ref.shape[0] - 1], group, turned, left, lat_dev, members)
 
@@ -387,8 +409,8 @@
 
     @pl.when(step == pl.num_programs(0) - 1)
     def _():
-        for copy in writes():
-            copy.wait()
+        for scale, ref in enumerate(new):
+            pltpu.make_async_copy(ref, new_out.at[:, scale], copy_sem.at[scale]).wait()
 
 
 def finish(new, summed, arrived, table):

time: 137 us -> 139 us (1.015)
  Pallas kernels: 136 us -> 138 us
    pallas_call x1, Pallas kernels: 127 us -> 130 us  [exchange(): pl.pallas_call(functools.partial(exchange_kernel, leaders, middle, count,...]
    pallas_call x1, Pallas kernels: 9.14 us -> 7.48 us  [finish(): pl.pallas_call(functools.partial(finish_kernel, group, members, scales),...]
where the time goes in v5:
time: 139 us
  Pallas kernels  138 us (99%)
    pallas_call x1, Pallas kernels, exchange(): pl.pallas_call(functools.partial(exchange_kernel, leaders, middle, count,...  130 us
    pallas_call x1, Pallas kernels, finish(): pl.pallas_call(functools.partial(finish_kernel, group, members, scales),...  7.48 us

profile of v5, /device:TPU:0, one launch (start us, length us, event | category | flops | bytes accessed | tf_op | source)
XLA Modules:
  0.0 138.6 jit_solution(14553899697201445136)
XLA Ops:
  0.6 130.3 %exchange.1 = (f32[20,50,2,640]{3,2,1,0:T(2,128)S(1)}, f32[20,50,2,640]{3,2,1,0:T(2,128)S(1)}, f32[20,50,2,640]{3,2,1,0:T(2,128)S(1)}, f32[20,56,1280]{2,1,0:T(8...) custom-call(s32[640]{0:T(1024)} %order_hbm.1, s32[640]{0:T(1024)} %waves_hbm.1, f32[3]{0:T(128)} %decay_hbm.1, ...), custom_call_target="tpu_custom_call" | custom-call | tf_op jit(solution)/shard_map/exchange/pallas_call | solution.py:343
  130.9 7.5 %finish.1 = (f32[20,50,1280]{2,1,0:T(8,128)}, f32[20,3,50,2,640]{4,3,2,1,0:T(2,128)}) custom-call(f32[20,50,2,640]{3,2,1,0:T(2,128)S(1)} %get-tuple-element.10.refs_0_, f32[20,50,2,640]{3,2,1,0:T(2,128)S(1)} %get-tuple-element.11.refs_1_, f32[20,50,2,640]{3,2,1,0:T(2,128)S(1)} %get-tuple-element.12.refs_2_, f32[20,56,1280]{2,1,0:T(8,128)S(1)} %get-tuple-element.13.refs_3_, ...), custom_call_target="tpu_custom_call" | custom-call | tf_op jit(solution)/shard_map/finish/pallas_call | solution.py:425

commit v6 on v5

--- a/solution.py
+++ b/solution.py
@@ -146,9 +146,8 @@
                 for copy in loads(slot + 1):
                     copy.start()
 
-            old_load, noise_load, basis_load = loads(slot)
-            old_load.wait()
-            noise_load.wait()
+            for copy in loads(slot):
+                copy.wait()
             side = lax.rem(slot, 2)
             wave_here = waves_ref[me * slots + slot]
             gains[...] = jnp.where(column + wave_here < width, pltpu.roll(base_gains[...], width - wave_here, axis=1), 0.0)
@@ -163,7 +162,6 @@
             for part in range(PARTS):
                 weights[part * HALF : part * HALF + members, :] = summed[:, part, :]
             high, low = split(weights[...])
-            basis_load.wait()
             basis_high, basis_low = split(basis[side])
             lanes = (((1,), (1,)), ((), ()))
             pair = lax.dot_general(basis_high, jnp.concatenate([high, low], axis=0), lanes, preferred_element_type=jnp.float32)

time: 139 us -> 134 us (0.964)
  Pallas kernels: 138 us -> 133 us
    pallas_call x1, Pallas kernels: 130 us -> 126 us  [exchange(): pl.pallas_call(functools.partial(exchange_kernel, leaders, middle, count,...]
where the time goes in v6:
time: 134 us
  Pallas kernels  133 us (99%)
    pallas_call x1, Pallas kernels, exchange(): pl.pallas_call(functools.partial(exchange_kernel, leaders, middle, count,...  126 us
    pallas_call x1, Pallas kernels, finish(): pl.pallas_call(functools.partial(finish_kernel, group, members, scales),...  7.48 us

profile of v6, /device:TPU:0, one launch (start us, length us, event | category | flops | bytes accessed | tf_op | source)
XLA Modules:
  0.0 133.8 jit_solution(980859735692953449)
XLA Ops:
  0.6 125.5 %exchange.1 = (f32[20,50,2,640]{3,2,1,0:T(2,128)S(1)}, f32[20,50,2,640]{3,2,1,0:T(2,128)S(1)}, f32[20,50,2,640]{3,2,1,0:T(2,128)S(1)}, f32[20,56,1280]{2,1,0:T(8...) custom-call(s32[640]{0:T(1024)} %order_hbm.1, s32[640]{0:T(1024)} %waves_hbm.1, f32[3]{0:T(128)} %decay_hbm.1, ...), custom_call_target="tpu_custom_call" | custom-call | tf_op jit(solution)/shard_map/exchange/pallas_call | solution.py:341
  126.1 7.5 %finish.1 = (f32[20,50,1280]{2,1,0:T(8,128)}, f32[20,3,50,2,640]{4,3,2,1,0:T(2,128)}) custom-call(f32[20,50,2,640]{3,2,1,0:T(2,128)S(1)} %get-tuple-element.10.refs_0_, f32[20,50,2,640]{3,2,1,0:T(2,128)S(1)} %get-tuple-element.11.refs_1_, f32[20,50,2,640]{3,2,1,0:T(2,128)S(1)} %get-tuple-element.12.refs_2_, f32[20,56,1280]{2,1,0:T(8,128)S(1)} %get-tuple-element.13.refs_3_, ...), custom_call_target="tpu_custom_call" | custom-call | tf_op jit(solution)/shard_map/finish/pallas_call | solution.py:423

commit v7 on v6

--- a/solution.py
+++ b/solution.py
@@ -42,7 +42,7 @@
 
 def plan(slots, lat_dev, members):
     if slots % 4 == 0 and slots >= 8:
-        sizes, size = (1, 1, 2), 4
+        sizes, size = (2, 2), 4
     elif slots > 4:
         sizes, size = (slots % 4,), 4
     else:

time: 134 us -> 132 us (0.985)
  Pallas kernels: 133 us -> 131 us
    pallas_call x1, Pallas kernels: 126 us -> 124 us  [exchange(): pl.pallas_call(functools.partial(exchange_kernel, leaders, middle, count,...]
where the time goes in v7:
time: 132 us
  Pallas kernels  131 us (99%)
    pallas_call x1, Pallas kernels, exchange(): pl.pallas_call(functools.partial(exchange_kernel, leaders, middle, count,...  124 us
    pallas_call x1, Pallas kernels, finish(): pl.pallas_call(functools.partial(finish_kernel, group, members, scales),...  7.48 us

profile of v7, /device:TPU:0, one launch (start us, length us, event | category | flops | bytes accessed | tf_op | source)
XLA Modules:
  0.0 132.0 jit_solution(13761736116675831314)
XLA Ops:
  0.6 123.7 %exchange.1 = (f32[20,50,2,640]{3,2,1,0:T(2,128)S(1)}, f32[20,50,2,640]{3,2,1,0:T(2,128)S(1)}, f32[20,50,2,640]{3,2,1,0:T(2,128)S(1)}, f32[20,56,1280]{2,1,0:T(8...) custom-call(s32[640]{0:T(1024)} %order_hbm.1, s32[640]{0:T(1024)} %waves_hbm.1, f32[3]{0:T(128)} %decay_hbm.1, ...), custom_call_target="tpu_custom_call" | custom-call | tf_op jit(solution)/shard_map/exchange/pallas_call | solution.py:341
  124.4 7.5 %finish.1 = (f32[20,50,1280]{2,1,0:T(8,128)}, f32[20,3,50,2,640]{4,3,2,1,0:T(2,128)}) custom-call(f32[20,50,2,640]{3,2,1,0:T(2,128)S(1)} %get-tuple-element.10.refs_0_, f32[20,50,2,640]{3,2,1,0:T(2,128)S(1)} %get-tuple-element.11.refs_1_, f32[20,50,2,640]{3,2,1,0:T(2,128)S(1)} %get-tuple-element.12.refs_2_, f32[20,56,1280]{2,1,0:T(8,128)S(1)} %get-tuple-element.13.refs_3_, ...), custom_call_target="tpu_custom_call" | custom-call | tf_op jit(solution)/shard_map/finish/pallas_call | solution.py:423
